TPU v7x, 32 devices: a whole 2x2x4 slice. The times are simulated.
32 devices in a mesh: gx: 4 (over z), gy: 4 (over x, core), gz: 2 (over y).
Axes of the slice: x: 2, y: 2, z: 4, core: 2. Of those that a mesh axis runs over, the one named last changes fastest.
Arguments:
- turbulence: float32 [128, 1024, 1024], P('gz', 'gx', 'gy'), may hold values from -6 to 6
Outputs:
- coefficients: float32 [128, 1024, 1024], P('gz', 'gx', 'gy')
All inputs are finite; a program needn't handle non-finite values.
Results may differ from a plain program's by a relative error of at most 0.000075.
Values sent between devices are 32-bit elements; how exact they have to be, the bound alone decides.
No kernel may reach another device: no remote copies, remote signals or barrier semaphores. Data moves between devices by JAX's collectives and lax.ppermute only.
A program may use at most 128 MiB of HBM per device.

v0:
```python
import jax
import jax.numpy as jnp
from jax import lax
from jax.sharding import PartitionSpec as P

LEVELS = 3


lift_alpha = -1.586134342059924
lift_beta = -0.052980118572961
lift_gamma = 0.882911075530934
lift_delta = 0.443506852043971
lift_zeta = 1.149604398860241
inverse_zeta = 1.0 / 1.149604398860241


def passed_along(value, axis, by):
    count = lax.axis_size(axis)
    return lax.ppermute(value, axis, [(i, (i + by) % count) for i in range(count)])


def first_plane(values, direction):
    return lax.slice_in_dim(values, 0, 1, 1, direction)


def last_plane(values, direction):
    length = values.shape[direction]
    return lax.slice_in_dim(values, length - 1, length, 1, direction)


def drop_first(values, direction):
    return lax.slice_in_dim(values, 1, values.shape[direction], 1, direction)


def drop_last(values, direction):
    return lax.slice_in_dim(values, 0, values.shape[direction] - 1, 1, direction)


def spread_table(half_length, offset):
    rows = lax.broadcasted_iota(jnp.int32, (half_length, 2 * half_length), 0)
    columns = lax.broadcasted_iota(jnp.int32, (half_length, 2 * half_length), 1)
    return (columns == 2 * rows + offset).astype(jnp.float32)


def spread_last(values, offset):
    table = spread_table(values.shape[2], offset)
    return jnp.einsum("abj,jk->abk", values, table, precision=lax.Precision.HIGHEST)


def join_pairs(even_part, odd_part, direction):
    if direction == 2:
        return spread_last(even_part, 0) + spread_last(odd_part, 1)
    merged = jnp.stack([even_part, odd_part], axis=direction + 1)
    new_shape = list(even_part.shape)
    new_shape[direction] = new_shape[direction] * 2
    return merged.reshape(new_shape)


def lift_core(values, direction, shifted_next, shifted_prev):
    length = values.shape[direction]
    even_part = lax.slice_in_dim(values, 0, length, 2, direction)
    odd_part = lax.slice_in_dim(values, 1, length, 2, direction)
    odd_part = odd_part + lift_alpha * (even_part + shifted_next(even_part))
    even_part = even_part + lift_beta * (shifted_prev(odd_part) + odd_part)
    odd_part = odd_part + lift_gamma * (even_part + shifted_next(even_part))
    even_part = even_part + lift_delta * (shifted_prev(odd_part) + odd_part)
    return join_pairs(even_part * lift_zeta, odd_part * inverse_zeta, direction)


def remote_edges(direction, fetcher):

    def shifted_next(operand):
        boundary = fetcher(first_plane(operand, direction), -1)
        return jnp.concatenate([drop_first(operand, direction), boundary], axis=direction)

    def shifted_prev(operand):
        boundary = fetcher(last_plane(operand, direction), 1)
        return jnp.concatenate([boundary, drop_last(operand, direction)], axis=direction)

    return (shifted_next, shifted_prev)


def rim_along_z(boundary, offset):
    return passed_along(boundary, "gz", offset)


def rim_along_x(boundary, offset):
    return passed_along(boundary, "gx", offset)


def rim_along_y(boundary, offset):
    return passed_along(boundary, "gy", offset)


def transform_level(current):
    for direction, fetcher in ((0, rim_along_z), (1, rim_along_x), (2, rim_along_y)):
        next_edge, prev_edge = remote_edges(direction, fetcher)
        current = lift_core(current, direction, next_edge, prev_edge)
    return current


def place_inner(finer, coarse):
    full_shape = finer.shape
    zeros_like = jnp.zeros_like(coarse)
    spread = join_pairs(coarse, zeros_like, 0)
    spread = join_pairs(spread, jnp.zeros_like(spread), 1)
    spread = spread_last(spread, 0)
    depth_index = lax.broadcasted_iota(jnp.int32, full_shape, 0)
    row_index = lax.broadcasted_iota(jnp.int32, full_shape, 1)
    column_index = lax.broadcasted_iota(jnp.int32, full_shape, 2)
    chosen = depth_index % 2 + row_index % 2 + column_index % 2 == 0
    return jnp.where(chosen, spread, finer)


def local(turbulence):
    finished_levels = []
    current = turbulence
    for level_index in range(LEVELS):
        finished = transform_level(current)
        finished_levels.append(finished)
        current = lax.slice(finished, (0, 0, 0), finished.shape, (2, 2, 2))
    result = finished_levels[-1]
    for finer in reversed(finished_levels[:-1]):
        result = place_inner(finer, result)
    return result


def solution(mesh):
    in_specs = (P("gz", "gx", "gy"),)
    out_specs = P("gz", "gx", "gy")
    return jax.shard_map(local, mesh=mesh, in_specs=in_specs, out_specs=out_specs, check_vma=False)
```

profile of v0, /device:TPU:0, one launch (start us, length us, event | category | flops | bytes accessed | tf_op | source)
XLA Modules:
  0.0 1381.6 jit_solution(8245018218360862579)
XLA Ops:
  7.9 5.4 collective-permute-done
  13.3 7.0 fusion.2
  27.9 9.3 fusion.4
  43.9 10.9 multiply_bitcast_fusion.1
  57.0 7.4 slice.375
  64.4 9.3 fusion.10
  73.6 11.7 pad_maximum_fusion
  85.3 36.1 %slice.286 = f32[64,128,256]{2,1,0:T(8,128)} slice(f32[64,256,256]{2,1,0:T(8,128)} %bitcast.91), slice={[0:64:1], [0:256:2], [0:256:1]} | slice | bytes 16777216 | tf_op jit(solution)/shard_map/slice | solution.py:61
  126.2 36.1 %slice.287 = f32[64,128,256]{2,1,0:T(8,128)} slice(f32[64,256,256]{2,1,0:T(8,128)} %bitcast.92), slice={[0:64:1], [1:256:2], [0:256:1]} | slice | bytes 16777216 | tf_op jit(solution)/shard_map/slice | solution.py:62
  162.3 8.2 slice.376
  170.4 7.1 fusion.12
  178.0 6.0 collective-permute-done.5
  184.0 10.5 fusion.14
  199.2 11.1 multiply_bitcast_fusion
  217.5 10.2 fusion.20
  227.7 6.8 pad_maximum_fusion.1
  234.5 19.6 %copy.37 = f32[64,128,2,256]{3,0,2,1:T(8,128)} copy(f32[64,128,2,256]{3,1,0,2:T(8,128)S(1)} %pad_maximum_fusion.1) | data formatting | bytes 33554432 | tf_op jit(solution)/shard_map/stack | solution.py:53
  254.1 280.4 %slice.296 = f32[64,256,128]{2,0,1:T(8,128)} slice(f32[64,256,256]{2,0,1:T(8,128)} %bitcast.93), slice={[0:64:1], [0:256:1], [0:256:2]} | slice | bytes 16777216 | tf_op jit(solution)/shard_map/slice | solution.py:61
  534.5 6.3 copy.38
  541.1 280.4 %slice.297 = f32[64,256,128]{2,0,1:T(8,128)} slice(f32[64,256,256]{2,0,1:T(8,128)} %bitcast.94), slice={[0:64:1], [0:256:1], [1:256:2]} | slice | bytes 16777216 | tf_op jit(solution)/shard_map/slice | solution.py:62
  821.5 8.9 slice.384
  830.4 7.5 copy.39
  837.8 12.5 fusion.22
  853.7 5.5 slice.386
  859.2 6.5 copy.40
  869.5 7.5 copy.41
  877.0 15.0 %fusion.24 = f32[64,256,128]{2,0,1:T(8,128)} fusion(f32[64,256,128]{2,0,1:T(8,128)} %slice.296, f32[64,256,128]{2,0,1:T(8,128)} %copy-done, f32[64,256,127]{2,0,1:T(8,128)} %bitcast.86, f32[64,256,1]{2,0,1:T(8,128)} %copy.41), kind=kLoop, calls=%fused_computation.38 | loop fusion | flops 8388608 | bytes 33554432 | tf_op jit(solution)/shard_map/add | solution.py:64
  892.0 6.3 copy.42
  898.4 8.9 slice.388
  907.3 7.6 copy.43
  914.8 18.9 %broadcast_multiply_fusion = (f32[64,256,128]{2,0,1:T(8,128)}, f32[64,256,128]{2,0,1:T(8,128)}) fusion(f32[64,256,128]{2,0,1:T(8,128)} %copy-done, f32[64,256,128]{2,0,1:T(8,128)} %fusion.24, f32[64,256,1]{2,0,1:T(8,128)} %copy.43, f32[64,256,127]{2,0,1:T(8,128)} %slice.388), kind=kLoop, calls=%fused_computation.51 | loop fusion | flops 10485760 | bytes 41943040 | tf_op jit(solution)/shard_map/mul | solution.py:67
  933.8 8.9 slice.390
  942.7 6.3 copy.44
  952.8 8.0 copy.45
  960.7 12.5 fusion.29
  973.3 16.3 %fusion.31 = f32[64,256,256]{2,1,0:T(8,128)} fusion(f32[64,256,128]{2,0,1:T(8,128)S(1)} %fusion.29, s32[128]{0:T(128)S(1)} %iota_multiply_fusion.2), kind=kOutput, calls=%fused_computation.47 | convolution fusion | flops 6442483712 | bytes 25166336 | tf_op jit(solution)/shard_map/abj,jk->abk/dot_general | solution.py:47
  989.6 21.4 %convolution_add_fusion = f32[64,256,256]{2,1,0:T(8,128)} fusion(f32[64,256,256]{2,1,0:T(8,128)} %fusion.31, f32[64,256,128]{2,0,1:T(8,128)} %get-tuple-element.17, s32[128]{0:T(128)S(1)} %broadcast_add_fusion.1), kind=kOutput, calls=%fused_computation.4 | convolution fusion | flops 6446678016 | bytes 41943552 | tf_op jit(solution)/shard_map/abj,jk->abk/dot_general | solution.py:47
  1011.0 72.3 %slice.306 = f32[32,128,128]{2,1,0:T(8,128)S(1)} slice(f32[64,256,256]{2,1,0:T(8,128)} %convolution_add_fusion), slice={[0:64:2], [0:256:2], [0:256:2]} | slice | bytes 4194304 | tf_op jit(solution)/shard_map/slice | solution.py:121
  1118.9 5.5 collective-permute-done.19
  1127.6 38.1 %slice.327 = f32[32,128,64]{2,0,1:T(8,128)S(1)} slice(f32[32,128,128]{2,0,1:T(8,128)} %bitcast.99), slice={[0:32:1], [0:128:1], [0:128:2]} | slice | bytes 2097152 | tf_op jit(solution)/shard_map/slice | solution.py:61
  1167.1 38.9 %slice.328 = f32[32,128,64]{2,0,1:T(8,128)} slice(f32[32,128,128]{2,0,1:T(8,128)} %bitcast.100), slice={[0:32:1], [0:128:1], [1:128:2]} | slice | bytes 2097152 | tf_op jit(solution)/shard_map/slice | solution.py:62
  1264.3 9.9 slice.337
  1316.0 6.0 slice.359
  1325.7 7.5 collective-permute-done.33
  1333.7 6.5 collective-permute-done.34
  1341.9 7.5 collective-permute-done.35
  1356.7 8.9 stack.95.clone
  1365.6 15.6 %fusion = f32[64,256,256]{2,1,0:T(8,128)} fusion(f32[64,256,256]{2,1,0:T(8,128)} %convolution_add_fusion, f32[64,256,128]{2,1,0:T(8,128)} %bitcast.107, s32[256]{0:T(256)S(1)} %get-tuple-element.27, s32[256]{0:T(256)S(1)} %get-tuple-element.28, s32[64]{0:T(128)S(1)} %get-tuple-element.29, s32[64]{0:T(128)S(1)} %get-tuple-element.30, ...), kind=kOutput, calls=%fused_computation.3 | convolution fusion | flops 6471843840 | bytes 41946432 | tf_op jit(solution)/shard_map/abj,jk->abk/dot_general | solution.py:47
  (201 shorter events, 205.3 us)
Async XLA Ops:
  4.0 9.4 collective-permute-start
  20.3 6.0 copy-start.3
  20.3 7.5 collective-permute-start.1
  37.2 6.7 collective-permute-start.2
  55.7 8.7 collective-permute-start.3
  122.5 47.9 %collective-permute-start.4 = (f32[64,1,256]{2,1,0:T(1,128)S(1)}, f32[64,1,256]{2,1,0:T(1,128)S(1)}, u32[]{:S(2)}, u32[]{:S(2)}) collective-permute-start(f32[64,1,256]{2,1,0:T(1,128)S(1)} %slice.377), channel_id=1, source_target_pairs={{0,24},{8,0},{16,8},{24,16},{1,25},{9,1},{17,9},{25,17},{2,26},{10... | collective-permute-start | bytes 196616 | tf_op jit(solution)/shard_map/ppermute | solution.py:19
  162.3 8.2 copy-start.2
  177.5 6.6 copy-start.1
  177.6 6.5 collective-permute-start.5
  194.5 4.6 collective-permute-start.6
  211.4 6.1 collective-permute-start.7
  540.9 289.5 %collective-permute-start.8 = (f32[64,256,1]{1,0,2:T(8,128)S(1)}, f32[64,256,1]{1,0,2:T(8,128)S(1)}, u32[]{:S(2)}, u32[]{:S(2)}) collective-permute-start(f32[64,256,1]{1,0,2:T(8,128)S(1)} %copy.38), channel_id=1, source_target_pairs={{0,6},{2,0},{4,2},{6,4},{1,7},{3,1},{5,3},{7,5},{8,14},{10,8},{12,... | collective-permute-start | bytes 196616 | tf_op jit(solution)/shard_map/ppermute | solution.py:19
  850.3 3.4 copy-start
  865.8 3.7 collective-permute-start.9
  898.3 8.9 collective-permute-start.10
  949.0 3.7 collective-permute-start.11
  1083.4 4.3 collective-permute-start.12
  1087.9 4.4 collective-permute-start.13
  1092.7 4.6 collective-permute-start.14
  1097.6 4.3 collective-permute-start.15
  1102.9 3.8 collective-permute-start.16
  1108.3 5.6 collective-permute-start.17
  1114.3 4.0 collective-permute-start.18
  1118.9 5.6 collective-permute-start.19
  1165.8 42.3 %copy-start.5 = (f32[32,128,64]{2,0,1:T(8,128)}, f32[32,128,64]{2,0,1:T(8,128)S(1)}, u32[]{:S(2)}) copy-start(f32[32,128,64]{2,0,1:T(8,128)S(1)} %slice.327) | copy-start | bytes 3145732
  1167.1 41.0 %collective-permute-start.20 = (f32[32,128,1]{1,0,2:T(8,128)S(1)}, f32[32,128,1]{1,0,2:T(8,128)S(1)}, u32[]{:S(2)}, u32[]{:S(2)}) collective-permute-start(f32[32,128,1]{1,0,2:T(8,128)S(1)} %copy.50), channel_id=1, source_target_pairs={{0,6},{2,0},{4,2},{6,4},{1,7},{3,1},{5,3},{7,5},{8,14},{10,8},{12,... | collective-permute-start | bytes 49160 | tf_op jit(solution)/shard_map/ppermute | solution.py:19
  1215.4 11.2 copy-start.4
  1220.1 3.6 collective-permute-start.21
  1232.3 2.0 collective-permute-start.22
  1242.5 1.4 copy-start.6
  1248.4 6.5 collective-permute-start.23
  1257.8 4.0 copy-start.7
  1274.3 4.0 collective-permute-start.24
  1278.3 4.0 collective-permute-start.25
  1282.4 4.1 collective-permute-start.26
  1286.6 4.0 collective-permute-start.27
  1291.1 3.7 collective-permute-start.28
  1294.9 5.5 collective-permute-start.29
  1300.5 3.7 collective-permute-start.30
  1304.3 5.5 collective-permute-start.31
  1315.7 7.0 collective-permute-start.32
  1324.3 8.9 collective-permute-start.33
  1333.4 6.8 collective-permute-start.34
  1340.6 8.8 collective-permute-start.35
where the time goes:
time: 1390 us; the launch traced here: 1380 us
  local copies, waits for them, and re-layouts  1000 us (72%)
  other arithmetic  178 us (13%)
  waiting for transfers between devices  110 us (8%)
  matrix products  64.6 us (5%)
  starting transfers between devices  26.9 us (2%)
    slice x9, local copies, waits for them, and re-layouts, lift_core(): even_part = lax.slice_in_dim(values, 0, length, 2, direction)  365 us
    slice x6, local copies, waits for them, and re-layouts, lift_core(): odd_part = lax.slice_in_dim(values, 1, length, 2, direction)  365 us
    ppermute x36, waiting for transfers between devices, passed_along(): lax.ppermute(value, axis, [(i, (i + by) % count) for i in range(count)])  110 us
    slice x2, local copies, waits for them, and re-layouts, local(): current = lax.slice(finished, (0, 0, 0), finished.shape, (2, 2, 2))  82.2 us
    dot_general x8, matrix products, spread_last(): jnp.einsum('abj,jk->abk', values, table, precision=lax.Precision.HIGHEST)  64.6 us
    another operation x18, other arithmetic, join_pairs(): merged = jnp.stack([even_part, odd_part], axis=direction + 1)  62.2 us
    ppermute x8, local copies, waits for them, and re-layouts, passed_along(): lax.ppermute(value, axis, [(i, (i + by) % count) for i in range(count)])  42.1 us
    mul x6, other arithmetic, lift_core(): return join_pairs(even_part * lift_zeta, odd_part * inverse_zeta, direction)  41 us
  transfers between devices with their start and end apart: 36, of which 28 were waited for; matrix products, arithmetic and copies ran while one was open for 31% of the time, Pallas kernels for 0%

commit v1 on v0

v1 whole, which is shorter than its diff:
```python
import functools

import jax
import jax.numpy as jnp
import numpy as np
from jax import lax
from jax.experimental import pallas as pl
from jax.experimental.pallas import tpu as pltpu
from jax.sharding import PartitionSpec as P

LEVELS = 3
ALPHA = -1.586134342059924
BETA = -0.052980118572961
GAMMA = 0.882911075530934
DELTA = 0.443506852043971
ZETA = 1.149604398860241
INVERSE_ZETA = 1.0 / 1.149604398860241
LANES = 128


def for_right(s_2, d_2, s_1, d_1):
    return d_1 + ALPHA * s_1, s_1 + BETA * (d_2 + ALPHA * (s_2 + s_1))


def for_left(s_0, d_0, s_1):
    return s_0, s_0 + BETA * (d_0 + ALPHA * (s_0 + s_1))


def lift(s, d, before, after, put):
    n = len(s)
    d1_last = before[0] + ALPHA * s[0]
    s1_last = before[1] + BETA * d1_last
    d2_last = None
    for i in range(n + 1):
        if i < n:
            s_next = s[i + 1] if i + 1 < n else after[0]
            d1 = d[i] + ALPHA * (s[i] + s_next)
            s1 = s[i] + BETA * (d1_last + d1)
        else:
            d1, s1 = None, after[1] + BETA * d1_last
        d2 = d1_last + GAMMA * (s1_last + s1)
        if i > 0:
            put(i - 1, (s1_last + DELTA * (d2_last + d2)) * ZETA, d2 * INVERSE_ZETA)
        d1_last, s1_last, d2_last = d1, s1, d2


def lifting_matrices(length):
    n = length // 2
    basis = np.eye(length + 4)
    s = [basis[2 * i] for i in range(n)]
    d = [basis[2 * i + 1] for i in range(n)]
    out = np.zeros((length + 4, length))

    def put(i, even, odd):
        out[:, 2 * i] = even
        out[:, 2 * i + 1] = odd

    rim = basis[length:]
    lift(s, d, (rim[0], rim[1]), (rim[2], rim[3]), put)
    return out[:length], out[length:]


def halves(a):
    high = a.astype(jnp.bfloat16)
    low = (a - high.astype(jnp.float32)).astype(jnp.bfloat16)
    return high, low


def np_halves(a):
    a = a.astype(np.float32)
    high = a.astype(jnp.bfloat16)
    low = (a - high.astype(np.float32)).astype(jnp.bfloat16)
    return high, low


class Sizes:
    def __init__(self, shape, step, valid):
        self.z, self.x, self.lanes = shape
        self.step = step
        self.y = valid
        self.out = max(LANES, -(-valid // LANES) * LANES)
        inner, rim = lifting_matrices(valid)
        full = np.zeros((self.lanes, self.out))
        full[: step * valid : step, :valid] = inner
        self.high, self.low = np_halves(full)
        edge = np.zeros((4, self.out))
        edge[:, :valid] = rim
        self.rim = edge.astype(np.float32)
        rim_high, rim_low = np_halves(edge)
        zeros = np.zeros((4, self.out), rim_high.dtype)
        self.rim_packed = np.concatenate([rim_high, rim_high, rim_low, zeros])


def dot(a, b):
    return jnp.dot(a, b, preferred_element_type=jnp.float32)


def times(rows, high_ref, low_ref):
    a, b = halves(rows)
    return dot(a, high_ref[...]) + dot(b, high_ref[...]) + dot(a, low_ref[...])


def whole(shape):
    return pl.BlockSpec(shape, lambda *_: (0,) * len(shape))


def edges_kernel(sizes, count, x_ref, left_ref, right_ref):
    step, n = sizes.step, sizes.y
    tile = (step * (n - 1)) // LANES * LANES
    low_lane = lax.broadcasted_iota(jnp.int32, (sizes.x, LANES), 1) < LANES // 2
    for p in range(count):
        both = x_ref[p, :, :LANES]
        if tile:
            both = jnp.where(low_lane, both, x_ref[p, :, tile : tile + LANES])
        both = both.T
        f = [both[step * k : step * k + 1] for k in range(3)]
        l = [both[step * (n - k) - tile : step * (n - k) - tile + 1] for k in (4, 3, 2, 1)]
        s, c = for_left(f[0], f[1], f[2])
        a, b = for_right(*l)
        left_ref[p, 0:1] = s
        left_ref[p, 1:2] = c
        right_ref[p, 0:1] = a
        right_ref[p, 1:2] = b


def edges(sizes, x):
    count = min(8, sizes.z)
    out = jax.ShapeDtypeStruct((sizes.z, 2, sizes.x), jnp.float32)
    spec = pl.BlockSpec((count, 2, sizes.x), lambda i: (i, 0, 0))
    return pl.pallas_call(
        functools.partial(edges_kernel, sizes, count),
        grid=(sizes.z // count,),
        in_specs=[pl.BlockSpec((count, sizes.x, sizes.lanes), lambda i: (i, 0, 0))],
        out_specs=[spec, spec],
        out_shape=[out, out],
        name="edges",
    )(x)


def rows_kernel(sizes, top_ref, bottom_ref, rim_rows_ref, high_ref, low_ref, rim_ref, left_ref, right_ref):
    z = sizes.z

    def across(ref, at):
        out = times(ref[...].reshape(z * 8, sizes.lanes), high_ref, low_ref)
        for h in range(4):
            column = rim_rows_ref[:, 8 * at : 8 * at + 8, h : h + 1].reshape(z * 8, 1)
            out = out + column * rim_ref[h : h + 1]
        return out.reshape(z, 8, sizes.out)

    top = across(top_ref, 0)
    bottom = across(bottom_ref, 1)
    s, c = for_left(top[:, 0:1], top[:, 1:2], top[:, 2:3])
    a, b = for_right(bottom[:, 4:5], bottom[:, 5:6], bottom[:, 6:7], bottom[:, 7:8])
    left_ref[:, 0:1] = s
    left_ref[:, 1:2] = c
    right_ref[:, 0:1] = a
    right_ref[:, 1:2] = b


def rows(sizes, x, rim_rows):
    z = sizes.z
    out = jax.ShapeDtypeStruct((z, 2, sizes.out), jnp.float32)
    last = sizes.x // 8 - 1
    return pl.pallas_call(
        functools.partial(rows_kernel, sizes),
        grid=(1,),
        in_specs=[
            pl.BlockSpec((z, 8, sizes.lanes), lambda i: (0, 0, 0)),
            pl.BlockSpec((z, 8, sizes.lanes), lambda i: (0, last, 0)),
            whole(rim_rows.shape),
            whole(sizes.high.shape),
            whole(sizes.low.shape),
            whole(sizes.rim.shape),
        ],
        out_specs=[whole(out.shape), whole(out.shape)],
        out_shape=[out, out],
        name="rows",
    )(x, x, rim_rows, sizes.high, sizes.low, sizes.rim)


def across_planes(sizes, count, refs, work):
    x_ref, yb_ref, ya_ref, xb_ref, xa_ref, high_ref, low_ref, rim_ref = refs
    n = sizes.x // 2
    at = lax.broadcasted_iota(jnp.int32, (n, LANES), 0)

    def shifted_next(v, edge):
        return jnp.where(at == n - 1, edge, pltpu.roll(v, n - 1, 0))

    def shifted_prev(v, edge):
        return jnp.where(at == 0, edge, pltpu.roll(v, 1, 0))

    for p in range(count):
        rim = jnp.concatenate([yb_ref[p], ya_ref[p]], axis=0)
        high = rim.astype(jnp.bfloat16).astype(jnp.float32)
        packed = jnp.concatenate([high, rim - high, high, jnp.zeros_like(high)], axis=0)
        across = times(x_ref[p], high_ref, low_ref) + dot(packed.T.astype(jnp.bfloat16), rim_ref[...])
        for c in range(sizes.out // LANES):
            lanes = slice(c * LANES, (c + 1) * LANES)
            work[p, c] = across[:, lanes]
            s = work[p, c, pl.ds(0, n, stride=2), :]
            d = work[p, c, pl.ds(1, n, stride=2), :]
            a, b = xb_ref[p, 0:1, lanes], xb_ref[p, 1:2, lanes]
            s_n, c_n = xa_ref[p, 0:1, lanes], xa_ref[p, 1:2, lanes]
            d1 = d + ALPHA * (s + shifted_next(s, s_n))
            d1_b = a + ALPHA * s[0:1]
            s1 = s + BETA * (shifted_prev(d1, d1_b) + d1)
            s1_b = b + BETA * d1_b
            s1_a = c_n + BETA * d1[n - 1 : n]
            d2 = d1 + GAMMA * (s1 + shifted_next(s1, s1_a))
            d2_b = d1_b + GAMMA * (s1_b + s1[0:1])
            s2 = s1 + DELTA * (shifted_prev(d2, d2_b) + d2)
            work[p, c, pl.ds(0, n, stride=2), :] = s2 * ZETA
            work[p, c, pl.ds(1, n, stride=2), :] = d2 * INVERSE_ZETA


def ends_kernel(sizes, *args):
    refs, left_ref, right_ref, work = args[:8], args[8], args[9], args[10]
    across_planes(sizes, 4, refs, work)
    for c in range(sizes.out // LANES):
        lanes = slice(c * LANES, (c + 1) * LANES)
        v = [work[p, c] for p in range(4)]

        @pl.when(pl.program_id(0) == 0)
        def _():
            left_ref[0, :, lanes], left_ref[1, :, lanes] = for_left(*v[:3])

        @pl.when(pl.program_id(0) == 1)
        def _():
            right_ref[0, :, lanes], right_ref[1, :, lanes] = for_right(*v)


def stream_kernel(sizes, steps, more, *args):
    refs, out_ref = args[:8], args[8]
    next_ref = args[9] if more else None
    work, state = args[-2:]
    step = pl.program_id(0)
    nx = sizes.x
    chunk = min(32, nx)

    @pl.when(step == 0)
    def _():
        state[...] = jnp.zeros_like(state)

    @pl.when(step < steps)
    def _():
        across_planes(sizes, 4, refs, work)

    @pl.when(step == steps)
    def _():
        work[...] = jnp.zeros_like(work)

    for c in range(sizes.out // LANES):
        lanes = slice(c * LANES, (c + 1) * LANES)
        for r in range(nx // chunk):
            at = slice(r * chunk, (r + 1) * chunk)
            s, d, d1_b, s1_b, d2_b = (state[k, c, at] for k in range(5))
            for q in range(2):
                s_n, d_n = work[2 * q, c, at], work[2 * q + 1, c, at]
                d1 = d + ALPHA * (s + s_n)
                s1 = s + BETA * (d1_b + d1)
                d2 = d1_b + GAMMA * (s1_b + s1)
                even = (s1_b + DELTA * (d2_b + d2)) * ZETA
                out_ref[2 * q, at, lanes] = even
                out_ref[2 * q + 1, at, lanes] = d2 * INVERSE_ZETA
                if more:
                    work[2 * q, c, at] = even
                s, d, d1_b, s1_b, d2_b = s_n, d_n, d1, s1, d2
            for k, v in enumerate((s, d, d1_b, s1_b, d2_b)):
                state[k, c, at] = v
        if more:
            for q in range(2):
                next_ref[q, :, lanes] = work[2 * q, c, pl.ds(0, nx // 2, stride=2), :]


def across_specs(sizes, place):
    return [
        pl.BlockSpec((4, sizes.x, sizes.lanes), place),
        pl.BlockSpec((4, 2, sizes.x), place),
        pl.BlockSpec((4, 2, sizes.x), place),
        pl.BlockSpec((4, 2, sizes.out), place),
        pl.BlockSpec((4, 2, sizes.out), place),
        whole(sizes.high.shape),
        whole(sizes.low.shape),
        whole(sizes.rim_packed.shape),
    ]


def cost(sizes, count):
    return pl.CostEstimate(
        flops=count * sizes.x * sizes.out * sizes.lanes * 8,
        bytes_accessed=count * sizes.x * (sizes.out + sizes.lanes) * 4,
        transcendentals=0,
    )


def ends(sizes, *operands):
    out = jax.ShapeDtypeStruct((2, sizes.x, sizes.out), jnp.float32)
    last = sizes.z // 4 - 1
    return pl.pallas_call(
        functools.partial(ends_kernel, sizes),
        grid=(2,),
        in_specs=across_specs(sizes, lambda i: (i * last, 0, 0)),
        out_specs=[whole(out.shape), whole(out.shape)],
        out_shape=[out, out],
        scratch_shapes=[pltpu.VMEM((4, sizes.out // LANES, sizes.x, LANES), jnp.float32)],
        cost_estimate=cost(sizes, 8),
        name="ends",
    )(*operands, sizes.high, sizes.low, sizes.rim_packed)


def stream(sizes, more, *operands):
    z, nx, width = sizes.z, sizes.x, sizes.out
    steps = z // 4
    behind = lambda i: (jnp.maximum(i - 1, 0), 0, 0)
    out_shape = [jax.ShapeDtypeStruct((z, nx, width), jnp.float32)]
    out_specs = [pl.BlockSpec((4, nx, width), behind)]
    if more:
        out_shape.append(jax.ShapeDtypeStruct((z // 2, nx // 2, width), jnp.float32))
        out_specs.append(pl.BlockSpec((2, nx // 2, width), behind))
    return pl.pallas_call(
        functools.partial(stream_kernel, sizes, steps, more),
        grid=(steps + 1,),
        in_specs=across_specs(sizes, lambda i: (jnp.minimum(i, steps - 1), 0, 0)),
        out_specs=out_specs,
        out_shape=out_shape,
        scratch_shapes=[
            pltpu.VMEM((4, width // LANES, nx, LANES), jnp.float32),
            pltpu.VMEM((5, width // LANES, nx, LANES), jnp.float32),
        ],
        cost_estimate=cost(sizes, z),
        name="stream",
    )(*operands, sizes.high, sizes.low, sizes.rim_packed)


def finish_kernel(sizes, more, zb_ref, za_ref, t_ref, *rest):
    if more:
        _, out_ref, next_ref, work = rest
    else:
        out_ref = rest[0]
    nx = sizes.x
    rim = lifting_matrices(sizes.z)[1]
    single = sizes.z == 4

    def apply(sides):
        for k in range(4):
            for c in range(sizes.out // LANES):
                lanes = slice(c * LANES, (c + 1) * LANES)
                total = t_ref[k, :, lanes]
                for h in range(4):
                    factor = rim[h, k if h < 2 else sizes.z - 4 + k]
                    if factor != 0.0 and h // 2 in sides:
                        ref = (zb_ref, za_ref)[h // 2]
                        total = total + float(factor) * ref[h % 2, :, lanes]
                out_ref[k, :, lanes] = total
                if more and k % 2 == 0:
                    work[c] = total
                    next_ref[k // 2, :, lanes] = work[c, pl.ds(0, nx // 2, stride=2), :]

    if single:
        apply((0, 1))
    else:
        pl.when(pl.program_id(0) == 0)(lambda: apply((0,)))
        pl.when(pl.program_id(0) == 1)(lambda: apply((1,)))


def finish(sizes, made, z_before, z_after):
    more = len(made) == 2
    z, nx, width = sizes.z, sizes.x, sizes.out
    last = z // 4 - 1
    place = lambda i: (i * last, 0, 0)
    specs = [pl.BlockSpec((4, nx, width), place)]
    scratch = []
    if more:
        specs.append(pl.BlockSpec((2, nx // 2, width), place))
        scratch.append(pltpu.VMEM((width // LANES, nx, LANES), jnp.float32))
    return pl.pallas_call(
        functools.partial(finish_kernel, sizes, more),
        grid=(min(2, last + 1),),
        in_specs=[whole((2, nx, width)), whole((2, nx, width))] + specs,
        out_specs=specs,
        out_shape=[jax.ShapeDtypeStruct(m.shape, m.dtype) for m in made],
        input_output_aliases={2 + k: k for k in range(len(made))},
        scratch_shapes=scratch,
        name="finish",
    )(z_before, z_after, *made)


def place_kernel(count, t_ref, r_ref, spread_ref, out_ref, work):
    nx, width = t_ref.shape[2], t_ref.shape[3]
    n = nx // 2
    even_lane = lax.broadcasted_iota(jnp.int32, (n, LANES), 1) % 2 == 0
    for p in range(count):
        rest = r_ref[p]
        high = rest.astype(jnp.bfloat16)
        rest = rest - high.astype(jnp.float32)
        middle, low = halves(rest)
        table = spread_ref[...]
        spread = dot(high, table) + dot(middle, table) + dot(low, table)
        for c in range(width // LANES):
            lanes = slice(c * LANES, (c + 1) * LANES)
            work[c] = t_ref[p, 0, :, lanes]
            even_rows = work[c, pl.ds(0, n, stride=2), :]
            work[c, pl.ds(0, n, stride=2), :] = jnp.where(even_lane, spread[:, lanes], even_rows)
            out_ref[p, 0, :, lanes] = work[c]


def place(t, r):
    z, nx, width = t.shape
    table = np.zeros((r.shape[2], width), np.float32)
    for j in range(min(r.shape[2], width // 2)):
        table[j, 2 * j] = 1.0
    count = min(8, z // 2)
    spec = pl.BlockSpec((count, 1, nx, width), lambda i: (i, 0, 0, 0))
    paired = t.reshape(z // 2, 2, nx, width)
    return pl.pallas_call(
        functools.partial(place_kernel, count),
        grid=(z // 2 // count,),
        in_specs=[
            spec,
            pl.BlockSpec((count,) + r.shape[1:], lambda i: (i, 0, 0)),
            whole(table.shape),
        ],
        out_specs=spec,
        out_shape=jax.ShapeDtypeStruct(paired.shape, jnp.float32),
        input_output_aliases={0: 0},
        scratch_shapes=[pltpu.VMEM((width // LANES, nx, LANES), jnp.float32)],
        name="place",
    )(paired, r, table.astype(jnp.bfloat16)).reshape(t.shape)


def exchange(axis, left, right):
    count = lax.axis_size(axis)
    before = lax.ppermute(right, axis, [(i, (i + 1) % count) for i in range(count)])
    after = lax.ppermute(left, axis, [(i, (i - 1) % count) for i in range(count)])
    return before, after


def level(sizes, x, more):
    y_before, y_after = exchange("gy", *edges(sizes, x))
    rim = jnp.concatenate([y_before, y_after], axis=1)
    rim_rows = jnp.concatenate([rim[:, :, :8], rim[:, :, -8:]], axis=2).swapaxes(1, 2)
    x_before, x_after = exchange("gx", *rows(sizes, x, rim_rows))
    sides = (y_before, y_after, x_before, x_after)
    z_before, z_after = exchange("gz", *ends(sizes, x, *sides))
    return finish(sizes, stream(sizes, more, x, *sides), z_before, z_after)


def local(turbulence):
    valid = turbulence.shape[2]
    current, step, done = turbulence, 1, []
    for index in range(LEVELS):
        more = index + 1 < LEVELS
        sizes = Sizes(current.shape, step, valid)
        made = level(sizes, current, more)
        done.append(made[0])
        if more:
            current, step, valid = made[1], 2, valid // 2
    result = done[-1]
    for finer in reversed(done[:-1]):
        result = place(finer, result)
    return result[:, :, : turbulence.shape[2]]


def solution(mesh):
    spec = P("gz", "gx", "gy")
    return jax.shard_map(local, mesh=mesh, in_specs=(spec,), out_specs=spec, check_vma=False)
```

time: 1390 us -> 146 us (0.11)
  local copies, waits for them, and re-layouts: 1000 us -> 9.02 us
  other arithmetic: 178 us -> 0.56 us
  Pallas kernels: 0 us -> 92.2 us
  waiting for transfers between devices: 110 us -> 19.1 us
  matrix products: 64.6 us -> 0 us
    slice x79 -> x0, local copies, waits for them, and re-layouts: 919 us -> none  [the longest x9 365 us: lift_core(): even_part = lax.slice_in_dim(values, 0, length, 2, direction)]
    pallas_call x0 -> x17, Pallas kernels: none -> 92.2 us  [the longest x3 41 us: stream(): pl.pallas_call(functools.partial(stream_kernel, sizes, steps, more), grid...]
    ppermute x36 -> x18, waiting for transfers between devices: 110 us -> 19.1 us  [the longest x9 15.1 us: exchange(): lax.ppermute(right, axis, [(i, (i + 1) % count) for i in range(count)])]
    add x21 -> x0, other arithmetic: 74.4 us -> none  [the longest x9 40.1 us: lift_core(): even_part = even_part + lift_beta * (shifted_prev(odd_part) + odd_part)]
    dot_general x8 -> x0, matrix products: 64.6 us -> none  [spread_last(): jnp.einsum('abj,jk->abk', values, table, precision=lax.Precision.HIGHEST)]
    another operation x18 -> x0, other arithmetic: 62.2 us -> none  [join_pairs(): merged = jnp.stack([even_part, odd_part], axis=direction + 1)]
    ppermute x8 -> x0, local copies, waits for them, and re-layouts: 42.1 us -> none  [passed_along(): lax.ppermute(value, axis, [(i, (i + by) % count) for i in range(count)])]
    mul x9 -> x0, other arithmetic: 41 us -> none  [the longest x6 41 us: lift_core(): return join_pairs(even_part * lift_zeta, odd_part * inverse_zeta, direction)]
  transfers between devices with their start and end apart: 36 -> 18, of which waited for: 28 -> 9; matrix products, arithmetic and copies ran while one was open for 31% -> 0% of each run, Pallas kernels for 0% -> 28%
where the time goes in v1:
time: 146 us; the launch traced here: 145 us
  Pallas kernels  92.2 us (63%)
  starting transfers between devices  23.5 us (16%)
  waiting for transfers between devices  19.1 us (13%)
  local copies, waits for them, and re-layouts  9.02 us (6%)
    pallas_call x3, Pallas kernels, stream(): pl.pallas_call(functools.partial(stream_kernel, sizes, steps, more), grid...  41 us
    ppermute x9, starting transfers between devices, exchange(): lax.ppermute(left, axis, [(i, (i - 1) % count) for i in range(count)])  15.9 us
    pallas_call x3, Pallas kernels, edges(): pl.pallas_call(functools.partial(edges_kernel, sizes, count), grid=(sizes...  15.6 us
    ppermute x9, waiting for transfers between devices, exchange(): lax.ppermute(right, axis, [(i, (i + 1) % count) for i in range(count)])  15.1 us
    pallas_call x2, Pallas kernels, place(): pl.pallas_call(functools.partial(place_kernel, count), grid=(z // 2 // co...  11.2 us
    pallas_call x3, Pallas kernels, ends(): pl.pallas_call(functools.partial(ends_kernel, sizes), grid=(2,), in_specs...  10 us
    ppermute x9, starting transfers between devices, exchange(): lax.ppermute(right, axis, [(i, (i + 1) % count) for i in range(count)])  7.63 us
    pallas_call x3, Pallas kernels, rows(): pl.pallas_call(functools.partial(rows_kernel, sizes), grid=(1,), in_specs...  7.33 us
  transfers between devices with their start and end apart: 18, of which 9 were waited for; matrix products, arithmetic and copies ran while one was open for 0% of the time, Pallas kernels for 28%

profile of v1, /device:TPU:0, one launch (start us, length us, event | category | flops | bytes accessed | tf_op | source)
XLA Modules:
  0.0 144.6 jit_solution(17111457333967702506)
XLA Ops:
  0.0 9.5 %edges.3 = (f32[64,2,256]{2,1,0:T(2,128)}, f32[64,2,256]{2,1,0:T(2,128)}) custom-call(f32[64,256,256]{2,1,0:T(8,128)} %args_0_.6), custom_call_target="tpu_custom_call" | custom-call | tf_op jit(solution)/shard_map/edges/pallas_call | solution.py:130
  10.0 1.9 %collective-permute-start.1 = (f32[64,2,256]{2,1,0:T(2,128)}, f32[64,2,256]{2,1,0:T(2,128)S(1)}, u32[]{:S(2)}, u32[]{:S(2)}) collective-permute-start(f32[64,2,256]{2,1,0:T(2,128)} %get-tuple-element.32), channel_id=1, source_target_pairs={{0,6},{2,0},{4,2},{6,4},{1,7},{3,1},{5,3},{7,5},{8,14},{10,8},{12,... | collective-permute-start | bytes 393224 | tf_op jit(solution)/shard_map/ppermute | solution.py:434
  11.9 2.9 %collective-permute-done.args_1_ = f32[64,2,256]{2,1,0:T(2,128)S(1)} collective-permute-done((f32[64,2,256]{2,1,0:T(2,128)}, f32[64,2,256]{2,1,0:T(2,128)S(1)}, u32[]{:S(2)}, u32[]{:S(2)}) %collective-permute-start) | collective-permute-done | bytes 131104 | tf_op jit(solution)/shard_map/ppermute | solution.py:433
  14.8 1.3 collective-permute-done.1.args_2_
  16.4 1.2 copy.31.rim_rows_ref
  17.6 3.3 %rows.3 = (f32[64,2,256]{2,1,0:T(2,128)}, f32[64,2,256]{2,1,0:T(2,128)}) custom-call(f32[64,256,256]{2,1,0:T(8,128)} %args_0_.6, f32[64,256,256]{2,1,0:T(8,128)} %args_0_.6, f32[64,16,4]{2,1,0:T(8,128)} %copy.31.rim_rows_ref, bf16[256,256]{1,0:T(8,128)(2,1)} %constant.28.clone.high_ref.args_5_, bf16[256,256]{1,0:T(8,128)(2,1)} %constant.29.clone.low_ref.args_6_, ...), custom_call_target="tpu_custom_call" | custom-call | tf_op jit(solution)/shard_map/rows/pallas_call | solution.py:164
  20.9 1.6 %collective-permute-start.2 = (f32[64,2,256]{2,1,0:T(2,128)}, f32[64,2,256]{2,1,0:T(2,128)S(1)}, u32[]{:S(2)}, u32[]{:S(2)}) collective-permute-start(f32[64,2,256]{2,1,0:T(2,128)} %get-tuple-element.33), channel_id=1, source_target_pairs={{0,8},{8,16},{16,24},{24,0},{1,9},{9,17},{17,25},{25,1},{2,10},{10... | collective-permute-start | bytes 393224 | tf_op jit(solution)/shard_map/ppermute | solution.py:433
  22.5 2.2 %collective-permute-start.3 = (f32[64,2,256]{2,1,0:T(2,128)}, f32[64,2,256]{2,1,0:T(2,128)S(1)}, u32[]{:S(2)}, u32[]{:S(2)}) collective-permute-start(f32[64,2,256]{2,1,0:T(2,128)} %get-tuple-element.34), channel_id=1, source_target_pairs={{0,24},{8,0},{16,8},{24,16},{1,25},{9,1},{17,9},{25,17},{2,26},{10... | collective-permute-start | bytes 393224 | tf_op jit(solution)/shard_map/ppermute | solution.py:434
  24.8 4.5 %collective-permute-done.2.args_3_ = f32[64,2,256]{2,1,0:T(2,128)S(1)} collective-permute-done((f32[64,2,256]{2,1,0:T(2,128)}, f32[64,2,256]{2,1,0:T(2,128)S(1)}, u32[]{:S(2)}, u32[]{:S(2)}) %collective-permute-start.2) | collective-permute-done | bytes 131104 | tf_op jit(solution)/shard_map/ppermute | solution.py:433
  29.2 2.5 %collective-permute-done.3.args_4_ = f32[64,2,256]{2,1,0:T(2,128)S(1)} collective-permute-done((f32[64,2,256]{2,1,0:T(2,128)}, f32[64,2,256]{2,1,0:T(2,128)S(1)}, u32[]{:S(2)}, u32[]{:S(2)}) %collective-permute-start.3) | collective-permute-done | bytes 131104 | tf_op jit(solution)/shard_map/ppermute | solution.py:434
  31.8 0.7 copy-done.9
  32.4 4.9 %ends.3 = (f32[2,256,256]{2,1,0:T(8,128)}, f32[2,256,256]{2,1,0:T(8,128)}) custom-call(f32[64,256,256]{2,1,0:T(8,128)} %args_0_.6, f32[64,2,256]{2,1,0:T(2,128)} %copy-done, f32[64,2,256]{2,1,0:T(2,128)} %copy-done.1, f32[64,2,256]{2,1,0:T(2,128)} %copy-done.8, f32[64,2,256]{2,1,0:T(2,128)} %copy-done.9, bf16[256,256]{1,0:T(8,128)(2,1)} %constant.28.clone.high_ref.args_5_, ...), custom_call_target="tpu_custom_call" | custom-call | flops 1073741824 | bytes 4194304 | tf_op jit(solution)/shard_map/ends/pallas_call | solution.py:299
  37.3 1.5 %collective-permute-start.4 = (f32[2,256,256]{2,1,0:T(8,128)}, f32[2,256,256]{2,1,0:T(8,128)S(1)}, u32[]{:S(2)}, u32[]{:S(2)}) collective-permute-start(f32[2,256,256]{2,1,0:T(8,128)} %get-tuple-element.35), channel_id=1, source_target_pairs={{0,1},{1,0},{2,3},{3,2},{4,5},{5,4},{6,7},{7,6},{8,9},{9,8},{10,11... | collective-permute-start | bytes 1572872 | tf_op jit(solution)/shard_map/ppermute | solution.py:433
  39.3 28.5 %stream.3 = (f32[64,256,256]{2,1,0:T(8,128)}, f32[32,128,256]{2,1,0:T(8,128)}) custom-call(f32[64,256,256]{2,1,0:T(8,128)} %args_0_.6, f32[64,2,256]{2,1,0:T(2,128)} %copy-done, f32[64,2,256]{2,1,0:T(2,128)} %copy-done.1, f32[64,2,256]{2,1,0:T(2,128)} %copy-done.8, f32[64,2,256]{2,1,0:T(2,128)} %copy-done.9, ...), custom_call_target="tpu_custom_call" | custom-call | flops 8589934592 | bytes 33554432 | tf_op jit(solution)/shard_map/stream/pallas_call | solution.py:320
  67.9 0.8 copy-done.4
  68.9 3.3 %finish.3 = (f32[64,256,256]{2,1,0:T(8,128)}, f32[32,128,256]{2,1,0:T(8,128)}) custom-call(f32[2,256,256]{2,1,0:T(8,128)} %copy-done.4, f32[2,256,256]{2,1,0:T(8,128)} %copy-done.5, f32[64,256,256]{2,1,0:T(8,128)} %get-tuple-element.37.t_ref, f32[32,128,256]{2,1,0:T(8,128)} %get-tuple-element.38.rest_0_), custom_call_target="tpu_custom_call", output_to_operand_aliasing={{0}: (2, {}), {1}: (3, {})} | custom-call | tf_op jit(solution)/shard_map/finish/pallas_call | solution.py:376
  72.1 4.1 %edges.4 = (f32[32,2,128]{2,1,0:T(2,128)}, f32[32,2,128]{2,1,0:T(2,128)}) custom-call(f32[32,128,256]{2,1,0:T(8,128)} %get-tuple-element.40.x_ref.top_ref.bottom_ref.args_0_), custom_call_target="tpu_custom_call" | custom-call | tf_op jit(solution)/shard_map/edges/pallas_call | solution.py:130
  76.3 1.7 %collective-permute-start.7 = (f32[32,2,128]{2,1,0:T(2,128)}, f32[32,2,128]{2,1,0:T(2,128)S(1)}, u32[]{:S(2)}, u32[]{:S(2)}) collective-permute-start(f32[32,2,128]{2,1,0:T(2,128)} %get-tuple-element.42), channel_id=1, source_target_pairs={{0,6},{2,0},{4,2},{6,4},{1,7},{3,1},{5,3},{7,5},{8,14},{10,8},{12,... | collective-permute-start | bytes 98312 | tf_op jit(solution)/shard_map/ppermute | solution.py:434
  78.0 1.8 %collective-permute-done.6.args_1_ = f32[32,2,128]{2,1,0:T(2,128)S(1)} collective-permute-done((f32[32,2,128]{2,1,0:T(2,128)}, f32[32,2,128]{2,1,0:T(2,128)S(1)}, u32[]{:S(2)}, u32[]{:S(2)}) %collective-permute-start.6) | collective-permute-done | bytes 32800 | tf_op jit(solution)/shard_map/ppermute | solution.py:433
  80.1 1.0 copy.32.rim_rows_ref
  81.1 2.2 %rows.4 = (f32[32,2,128]{2,1,0:T(2,128)}, f32[32,2,128]{2,1,0:T(2,128)}) custom-call(f32[32,128,256]{2,1,0:T(8,128)} %get-tuple-element.40.x_ref.top_ref.bottom_ref.args_0_, f32[32,128,256]{2,1,0:T(8,128)} %get-tuple-element.40.x_ref.top_ref.bottom_ref.args_0_, f32[32,16,4]{2,1,0:T(8,128)} %copy.32.rim_rows_ref, ...), custom_call_target="tpu_custom_call" | custom-call | tf_op jit(solution)/shard_map/rows/pallas_call | solution.py:164
  83.3 1.0 collective-permute-start.8
  84.3 2.9 %collective-permute-start.9 = (f32[32,2,128]{2,1,0:T(2,128)}, f32[32,2,128]{2,1,0:T(2,128)S(1)}, u32[]{:S(2)}, u32[]{:S(2)}) collective-permute-start(f32[32,2,128]{2,1,0:T(2,128)} %get-tuple-element.44), channel_id=1, source_target_pairs={{0,24},{8,0},{16,8},{24,16},{1,25},{9,1},{17,9},{25,17},{2,26},{10... | collective-permute-start | bytes 98312 | tf_op jit(solution)/shard_map/ppermute | solution.py:434
  87.2 2.4 %collective-permute-done.8.args_3_ = f32[32,2,128]{2,1,0:T(2,128)S(1)} collective-permute-done((f32[32,2,128]{2,1,0:T(2,128)}, f32[32,2,128]{2,1,0:T(2,128)S(1)}, u32[]{:S(2)}, u32[]{:S(2)}) %collective-permute-start.8) | collective-permute-done | bytes 32800 | tf_op jit(solution)/shard_map/ppermute | solution.py:433
  89.5 0.6 copy-done.10
  90.1 0.6 copy-done.11
  90.7 2.9 %ends.4 = (f32[2,128,128]{2,1,0:T(8,128)}, f32[2,128,128]{2,1,0:T(8,128)}) custom-call(f32[32,128,256]{2,1,0:T(8,128)} %get-tuple-element.40.x_ref.top_ref.bottom_ref.args_0_, f32[32,2,128]{2,1,0:T(2,128)} %copy-done.2, f32[32,2,128]{2,1,0:T(2,128)} %copy-done.3, f32[32,2,128]{2,1,0:T(2,128)} %copy-done.10, f32[32,2,128]{2,1,0:T(2,128)} %copy-done.11, ...), custom_call_target="tpu_custom_call" | custom-call | flops 268435456 | bytes 1572864 | tf_op jit(solution)/shard_map/ends/pallas_call | solution.py:299
  93.6 1.5 %collective-permute-start.10 = (f32[2,128,128]{2,1,0:T(8,128)}, f32[2,128,128]{2,1,0:T(8,128)S(1)}, u32[]{:S(2)}, u32[]{:S(2)}) collective-permute-start(f32[2,128,128]{2,1,0:T(8,128)} %get-tuple-element.45), channel_id=1, source_target_pairs={{0,1},{1,0},{2,3},{3,2},{4,5},{5,4},{6,7},{7,6},{8,9},{9,8},{10,11... | collective-permute-start | bytes 393224 | tf_op jit(solution)/shard_map/ppermute | solution.py:433
  95.6 8.6 %stream.4 = (f32[32,128,128]{2,1,0:T(8,128)}, f32[16,64,128]{2,1,0:T(8,128)}) custom-call(f32[32,128,256]{2,1,0:T(8,128)} %get-tuple-element.40.x_ref.top_ref.bottom_ref.args_0_, f32[32,2,128]{2,1,0:T(2,128)} %copy-done.2, f32[32,2,128]{2,1,0:T(2,128)} %copy-done.3, f32[32,2,128]{2,1,0:T(2,128)} %copy-done.10, f32[32,2,128]{2,1,0:T(2,128)} %copy-done.11, ...), custom_call_target="tpu_custom_call" | custom-call | flops 1073741824 | bytes 6291456 | tf_op jit(solution)/shard_map/stream/pallas_call | solution.py:320
  104.3 0.6 copy-done.12
  104.9 2.0 %finish.4 = (f32[32,128,128]{2,1,0:T(8,128)}, f32[16,64,128]{2,1,0:T(8,128)}) custom-call(f32[2,128,128]{2,1,0:T(8,128)} %copy-done.12, f32[2,128,128]{2,1,0:T(8,128)} %copy-done.13, f32[32,128,128]{2,1,0:T(8,128)} %get-tuple-element.47.t_ref, f32[16,64,128]{2,1,0:T(8,128)} %get-tuple-element.48.rest_0_), custom_call_target="tpu_custom_call", output_to_operand_aliasing={{0}: (2, {}), {1}: (3, {})} | custom-call | tf_op jit(solution)/shard_map/finish/pallas_call | solution.py:376
  106.9 2.0 %edges.5 = (f32[16,2,64]{2,1,0:T(2,128)}, f32[16,2,64]{2,1,0:T(2,128)}) custom-call(f32[16,64,128]{2,1,0:T(8,128)} %get-tuple-element.50.x_ref.top_ref.bottom_ref.args_0_), custom_call_target="tpu_custom_call" | custom-call | tf_op jit(solution)/shard_map/edges/pallas_call | solution.py:130
  108.9 1.7 %collective-permute-start.13 = (f32[16,2,64]{2,1,0:T(2,128)}, f32[16,2,64]{2,1,0:T(2,128)S(1)}, u32[]{:S(2)}, u32[]{:S(2)}) collective-permute-start(f32[16,2,64]{2,1,0:T(2,128)} %get-tuple-element.52), channel_id=1, source_target_pairs={{0,6},{2,0},{4,2},{6,4},{1,7},{3,1},{5,3},{7,5},{8,14},{10,8},{12,... | collective-permute-start | bytes 24584 | tf_op jit(solution)/shard_map/ppermute | solution.py:434
  110.7 1.6 %collective-permute-done.12.args_1_ = f32[16,2,64]{2,1,0:T(2,128)S(1)} collective-permute-done((f32[16,2,64]{2,1,0:T(2,128)}, f32[16,2,64]{2,1,0:T(2,128)S(1)}, u32[]{:S(2)}, u32[]{:S(2)}) %collective-permute-start.12) | collective-permute-done | bytes 8224 | tf_op jit(solution)/shard_map/ppermute | solution.py:433
  112.5 0.8 copy.33.rim_rows_ref
  113.3 1.9 %rows.5 = (f32[16,2,128]{2,1,0:T(2,128)}, f32[16,2,128]{2,1,0:T(2,128)}) custom-call(f32[16,64,128]{2,1,0:T(8,128)} %get-tuple-element.50.x_ref.top_ref.bottom_ref.args_0_, f32[16,64,128]{2,1,0:T(8,128)} %get-tuple-element.50.x_ref.top_ref.bottom_ref.args_0_, f32[16,16,4]{2,1,0:T(8,128)} %copy.33.rim_rows_ref, ...), custom_call_target="tpu_custom_call" | custom-call | tf_op jit(solution)/shard_map/rows/pallas_call | solution.py:164
  115.2 3.8 %collective-permute-start.15 = (f32[16,2,128]{2,1,0:T(2,128)}, f32[16,2,128]{2,1,0:T(2,128)S(1)}, u32[]{:S(2)}, u32[]{:S(2)}) collective-permute-start(f32[16,2,128]{2,1,0:T(2,128)} %get-tuple-element.54), channel_id=1, source_target_pairs={{0,24},{8,0},{16,8},{24,16},{1,25},{9,1},{17,9},{25,17},{2,26},{10... | collective-permute-start | bytes 49160 | tf_op jit(solution)/shard_map/ppermute | solution.py:434
  119.0 2.0 %collective-permute-done.14.args_3_ = f32[16,2,128]{2,1,0:T(2,128)S(1)} collective-permute-done((f32[16,2,128]{2,1,0:T(2,128)}, f32[16,2,128]{2,1,0:T(2,128)S(1)}, u32[]{:S(2)}, u32[]{:S(2)}) %collective-permute-start.14) | collective-permute-done | bytes 16416 | tf_op jit(solution)/shard_map/ppermute | solution.py:433
  121.0 0.6 copy-done.14
  121.6 0.6 copy-done.15
  122.2 2.3 %ends.5 = (f32[2,64,128]{2,1,0:T(8,128)}, f32[2,64,128]{2,1,0:T(8,128)}) custom-call(f32[16,64,128]{2,1,0:T(8,128)} %get-tuple-element.50.x_ref.top_ref.bottom_ref.args_0_, f32[16,2,64]{2,1,0:T(2,128)} %copy-done.6, f32[16,2,64]{2,1,0:T(2,128)} %copy-done.7, f32[16,2,128]{2,1,0:T(2,128)} %copy-done.14, f32[16,2,128]{2,1,0:T(2,128)} %copy-done.15, ...), custom_call_target="tpu_custom_call" | custom-call | flops 67108864 | bytes 524288 | tf_op jit(solution)/shard_map/ends/pallas_call | solution.py:299
  124.5 1.5 %collective-permute-start.16 = (f32[2,64,128]{2,1,0:T(8,128)}, f32[2,64,128]{2,1,0:T(8,128)S(1)}, u32[]{:S(2)}, u32[]{:S(2)}) collective-permute-start(f32[2,64,128]{2,1,0:T(8,128)} %get-tuple-element.55), channel_id=1, source_target_pairs={{0,1},{1,0},{2,3},{3,2},{4,5},{5,4},{6,7},{7,6},{8,9},{9,8},{10,11... | collective-permute-start | bytes 196616 | tf_op jit(solution)/shard_map/ppermute | solution.py:433
  126.5 3.9 %stream.5.t_ref = f32[16,64,128]{2,1,0:T(8,128)} custom-call(f32[16,64,128]{2,1,0:T(8,128)} %get-tuple-element.50.x_ref.top_ref.bottom_ref.args_0_, f32[16,2,64]{2,1,0:T(2,128)} %copy-done.6, f32[16,2,64]{2,1,0:T(2,128)} %copy-done.7, f32[16,2,128]{2,1,0:T(2,128)} %copy-done.14, f32[16,2,128]{2,1,0:T(2,128)} %copy-done.15, ...), custom_call_target="tpu_custom_call" | custom-call | flops 134217728 | bytes 1048576 | tf_op jit(solution)/shard_map/stream/pallas_call | solution.py:320
  130.5 0.6 copy-done.16
  131.1 0.6 copy-done.17
  131.7 1.7 %finish.5.r_ref = f32[16,64,128]{2,1,0:T(8,128)} custom-call(f32[2,64,128]{2,1,0:T(8,128)} %copy-done.16, f32[2,64,128]{2,1,0:T(8,128)} %copy-done.17, f32[16,64,128]{2,1,0:T(8,128)} %stream.5.t_ref), custom_call_target="tpu_custom_call", output_to_operand_aliasing={{}: (2, {})} | custom-call | tf_op jit(solution)/shard_map/finish/pallas_call | solution.py:376
  133.4 2.7 %place.2 = f32[16,2,128,128]{3,2,1,0:T(8,128)} custom-call(f32[16,2,128,128]{3,2,1,0:T(8,128)} %bitcast.11, f32[16,64,128]{2,1,0:T(8,128)} %finish.5.r_ref, bf16[128,128]{1,0:T(8,128)(2,1)} %constant.40.clone.spread_ref), custom_call_target="tpu_custom_call", output_to_operand_aliasing={{}: (0, {})} | custom-call | tf_op jit(solution)/shard_map/place/pallas_call | solution.py:415
  136.1 8.5 %place.3 = f32[32,2,256,256]{3,2,1,0:T(8,128)} custom-call(f32[32,2,256,256]{3,2,1,0:T(8,128)} %bitcast.10, f32[32,128,128]{2,1,0:T(8,128)} %bitcast.12, bf16[128,256]{1,0:T(8,128)(2,1)} %constant.41.clone.spread_ref), custom_call_target="tpu_custom_call", output_to_operand_aliasing={{}: (0, {})} | custom-call | tf_op jit(solution)/shard_map/place/pallas_call | solution.py:415
  (50 shorter events, 3.0 us)
Async XLA Ops:
  9.5 5.3 %collective-permute-start = (f32[64,2,256]{2,1,0:T(2,128)}, f32[64,2,256]{2,1,0:T(2,128)S(1)}, u32[]{:S(2)}, u32[]{:S(2)}) collective-permute-start(f32[64,2,256]{2,1,0:T(2,128)} %get-tuple-element.31), channel_id=1, source_target_pairs={{0,2},{2,4},{4,6},{6,0},{1,3},{3,5},{5,7},{7,1},{8,10},{10,12},{12... | collective-permute-start | bytes 393224 | tf_op jit(solution)/shard_map/ppermute | solution.py:433
  10.0 6.1 %collective-permute-start.1 = (f32[64,2,256]{2,1,0:T(2,128)}, f32[64,2,256]{2,1,0:T(2,128)S(1)}, u32[]{:S(2)}, u32[]{:S(2)}) collective-permute-start(f32[64,2,256]{2,1,0:T(2,128)} %get-tuple-element.32), channel_id=1, source_target_pairs={{0,6},{2,0},{4,2},{6,4},{1,7},{3,1},{5,3},{7,5},{8,14},{10,8},{12,... | collective-permute-start | bytes 393224 | tf_op jit(solution)/shard_map/ppermute | solution.py:434
  14.8 6.1 %copy-start = (f32[64,2,256]{2,1,0:T(2,128)}, f32[64,2,256]{2,1,0:T(2,128)S(1)}, u32[]{:S(2)}) copy-start(f32[64,2,256]{2,1,0:T(2,128)S(1)} %collective-permute-done.args_1_) | copy-start | bytes 393220
  16.1 4.8 %copy-start.1 = (f32[64,2,256]{2,1,0:T(2,128)}, f32[64,2,256]{2,1,0:T(2,128)S(1)}, u32[]{:S(2)}) copy-start(f32[64,2,256]{2,1,0:T(2,128)S(1)} %collective-permute-done.1.args_2_) | copy-start | bytes 393220
  20.9 8.3 %collective-permute-start.2 = (f32[64,2,256]{2,1,0:T(2,128)}, f32[64,2,256]{2,1,0:T(2,128)S(1)}, u32[]{:S(2)}, u32[]{:S(2)}) collective-permute-start(f32[64,2,256]{2,1,0:T(2,128)} %get-tuple-element.33), channel_id=1, source_target_pairs={{0,8},{8,16},{16,24},{24,0},{1,9},{9,17},{17,25},{25,1},{2,10},{10... | collective-permute-start | bytes 393224 | tf_op jit(solution)/shard_map/ppermute | solution.py:433
  22.5 9.2 %collective-permute-start.3 = (f32[64,2,256]{2,1,0:T(2,128)}, f32[64,2,256]{2,1,0:T(2,128)S(1)}, u32[]{:S(2)}, u32[]{:S(2)}) collective-permute-start(f32[64,2,256]{2,1,0:T(2,128)} %get-tuple-element.34), channel_id=1, source_target_pairs={{0,24},{8,0},{16,8},{24,16},{1,25},{9,1},{17,9},{25,17},{2,26},{10... | collective-permute-start | bytes 393224 | tf_op jit(solution)/shard_map/ppermute | solution.py:434
  29.2 2.5 %copy-start.8 = (f32[64,2,256]{2,1,0:T(2,128)}, f32[64,2,256]{2,1,0:T(2,128)S(1)}, u32[]{:S(2)}) copy-start(f32[64,2,256]{2,1,0:T(2,128)S(1)} %collective-permute-done.2.args_3_) | copy-start | bytes 393220
  31.8 0.7 copy-start.9
  37.3 30.5 %collective-permute-start.4 = (f32[2,256,256]{2,1,0:T(8,128)}, f32[2,256,256]{2,1,0:T(8,128)S(1)}, u32[]{:S(2)}, u32[]{:S(2)}) collective-permute-start(f32[2,256,256]{2,1,0:T(8,128)} %get-tuple-element.35), channel_id=1, source_target_pairs={{0,1},{1,0},{2,3},{3,2},{4,5},{5,4},{6,7},{7,6},{8,9},{9,8},{10,11... | collective-permute-start | bytes 1572872 | tf_op jit(solution)/shard_map/ppermute | solution.py:433
  38.8 29.0 %collective-permute-start.5 = (f32[2,256,256]{2,1,0:T(8,128)}, f32[2,256,256]{2,1,0:T(8,128)S(1)}, u32[]{:S(2)}, u32[]{:S(2)}) collective-permute-start(f32[2,256,256]{2,1,0:T(8,128)} %get-tuple-element.36), channel_id=1, source_target_pairs={{0,1},{1,0},{2,3},{3,2},{4,5},{5,4},{6,7},{7,6},{8,9},{9,8},{10,11... | collective-permute-start | bytes 1572872 | tf_op jit(solution)/shard_map/ppermute | solution.py:434
  67.8 0.8 copy-start.4
  67.9 1.0 copy-start.5
  76.3 3.6 %collective-permute-start.6 = (f32[32,2,128]{2,1,0:T(2,128)}, f32[32,2,128]{2,1,0:T(2,128)S(1)}, u32[]{:S(2)}, u32[]{:S(2)}) collective-permute-start(f32[32,2,128]{2,1,0:T(2,128)} %get-tuple-element.41), channel_id=1, source_target_pairs={{0,2},{2,4},{4,6},{6,0},{1,3},{3,5},{5,7},{7,1},{8,10},{10,12},{12... | collective-permute-start | bytes 98312 | tf_op jit(solution)/shard_map/ppermute | solution.py:433
  76.3 3.7 %collective-permute-start.7 = (f32[32,2,128]{2,1,0:T(2,128)}, f32[32,2,128]{2,1,0:T(2,128)S(1)}, u32[]{:S(2)}, u32[]{:S(2)}) collective-permute-start(f32[32,2,128]{2,1,0:T(2,128)} %get-tuple-element.42), channel_id=1, source_target_pairs={{0,6},{2,0},{4,2},{6,4},{1,7},{3,1},{5,3},{7,5},{8,14},{10,8},{12,... | collective-permute-start | bytes 98312 | tf_op jit(solution)/shard_map/ppermute | solution.py:434
  79.8 3.5 %copy-start.2 = (f32[32,2,128]{2,1,0:T(2,128)}, f32[32,2,128]{2,1,0:T(2,128)S(1)}, u32[]{:S(2)}) copy-start(f32[32,2,128]{2,1,0:T(2,128)S(1)} %collective-permute-done.6.args_1_) | copy-start | bytes 98308
  79.9 3.4 %copy-start.3 = (f32[32,2,128]{2,1,0:T(2,128)}, f32[32,2,128]{2,1,0:T(2,128)S(1)}, u32[]{:S(2)}) copy-start(f32[32,2,128]{2,1,0:T(2,128)S(1)} %collective-permute-done.7.args_2_) | copy-start | bytes 98308
  83.3 6.2 %collective-permute-start.8 = (f32[32,2,128]{2,1,0:T(2,128)}, f32[32,2,128]{2,1,0:T(2,128)S(1)}, u32[]{:S(2)}, u32[]{:S(2)}) collective-permute-start(f32[32,2,128]{2,1,0:T(2,128)} %get-tuple-element.43), channel_id=1, source_target_pairs={{0,8},{8,16},{16,24},{24,0},{1,9},{9,17},{17,25},{25,1},{2,10},{10... | collective-permute-start | bytes 98312 | tf_op jit(solution)/shard_map/ppermute | solution.py:433
  84.3 5.2 %collective-permute-start.9 = (f32[32,2,128]{2,1,0:T(2,128)}, f32[32,2,128]{2,1,0:T(2,128)S(1)}, u32[]{:S(2)}, u32[]{:S(2)}) collective-permute-start(f32[32,2,128]{2,1,0:T(2,128)} %get-tuple-element.44), channel_id=1, source_target_pairs={{0,24},{8,0},{16,8},{24,16},{1,25},{9,1},{17,9},{25,17},{2,26},{10... | collective-permute-start | bytes 98312 | tf_op jit(solution)/shard_map/ppermute | solution.py:434
  89.5 0.6 copy-start.10
  90.1 0.6 copy-start.11
  93.6 10.6 %collective-permute-start.10 = (f32[2,128,128]{2,1,0:T(8,128)}, f32[2,128,128]{2,1,0:T(8,128)S(1)}, u32[]{:S(2)}, u32[]{:S(2)}) collective-permute-start(f32[2,128,128]{2,1,0:T(8,128)} %get-tuple-element.45), channel_id=1, source_target_pairs={{0,1},{1,0},{2,3},{3,2},{4,5},{5,4},{6,7},{7,6},{8,9},{9,8},{10,11... | collective-permute-start | bytes 393224 | tf_op jit(solution)/shard_map/ppermute | solution.py:433
  95.1 9.1 %collective-permute-start.11 = (f32[2,128,128]{2,1,0:T(8,128)}, f32[2,128,128]{2,1,0:T(8,128)S(1)}, u32[]{:S(2)}, u32[]{:S(2)}) collective-permute-start(f32[2,128,128]{2,1,0:T(8,128)} %get-tuple-element.46), channel_id=1, source_target_pairs={{0,1},{1,0},{2,3},{3,2},{4,5},{5,4},{6,7},{7,6},{8,9},{9,8},{10,11... | collective-permute-start | bytes 393224 | tf_op jit(solution)/shard_map/ppermute | solution.py:434
  104.2 0.7 copy-start.12
  104.2 0.7 copy-start.13
  108.9 3.4 %collective-permute-start.12 = (f32[16,2,64]{2,1,0:T(2,128)}, f32[16,2,64]{2,1,0:T(2,128)S(1)}, u32[]{:S(2)}, u32[]{:S(2)}) collective-permute-start(f32[16,2,64]{2,1,0:T(2,128)} %get-tuple-element.51), channel_id=1, source_target_pairs={{0,2},{2,4},{4,6},{6,0},{1,3},{3,5},{5,7},{7,1},{8,10},{10,12},{12... | collective-permute-start | bytes 24584 | tf_op jit(solution)/shard_map/ppermute | solution.py:433
  108.9 3.4 %collective-permute-start.13 = (f32[16,2,64]{2,1,0:T(2,128)}, f32[16,2,64]{2,1,0:T(2,128)S(1)}, u32[]{:S(2)}, u32[]{:S(2)}) collective-permute-start(f32[16,2,64]{2,1,0:T(2,128)} %get-tuple-element.52), channel_id=1, source_target_pairs={{0,6},{2,0},{4,2},{6,4},{1,7},{3,1},{5,3},{7,5},{8,14},{10,8},{12,... | collective-permute-start | bytes 24584 | tf_op jit(solution)/shard_map/ppermute | solution.py:434
  112.3 8.7 %copy-start.6 = (f32[16,2,64]{2,1,0:T(2,128)}, f32[16,2,64]{2,1,0:T(2,128)S(1)}, u32[]{:S(2)}) copy-start(f32[16,2,64]{2,1,0:T(2,128)S(1)} %collective-permute-done.12.args_1_) | copy-start | bytes 24580
  112.3 8.7 %copy-start.7 = (f32[16,2,64]{2,1,0:T(2,128)}, f32[16,2,64]{2,1,0:T(2,128)S(1)}, u32[]{:S(2)}) copy-start(f32[16,2,64]{2,1,0:T(2,128)S(1)} %collective-permute-done.13.args_2_) | copy-start | bytes 24580
  115.2 5.8 %collective-permute-start.14 = (f32[16,2,128]{2,1,0:T(2,128)}, f32[16,2,128]{2,1,0:T(2,128)S(1)}, u32[]{:S(2)}, u32[]{:S(2)}) collective-permute-start(f32[16,2,128]{2,1,0:T(2,128)} %get-tuple-element.53), channel_id=1, source_target_pairs={{0,8},{8,16},{16,24},{24,0},{1,9},{9,17},{17,25},{25,1},{2,10},{10... | collective-permute-start | bytes 49160 | tf_op jit(solution)/shard_map/ppermute | solution.py:433
  115.2 5.9 %collective-permute-start.15 = (f32[16,2,128]{2,1,0:T(2,128)}, f32[16,2,128]{2,1,0:T(2,128)S(1)}, u32[]{:S(2)}, u32[]{:S(2)}) collective-permute-start(f32[16,2,128]{2,1,0:T(2,128)} %get-tuple-element.54), channel_id=1, source_target_pairs={{0,24},{8,0},{16,8},{24,16},{1,25},{9,1},{17,9},{25,17},{2,26},{10... | collective-permute-start | bytes 49160 | tf_op jit(solution)/shard_map/ppermute | solution.py:434
  121.0 0.6 copy-start.14
  121.6 0.6 copy-start.15
  124.5 6.0 %collective-permute-start.16 = (f32[2,64,128]{2,1,0:T(8,128)}, f32[2,64,128]{2,1,0:T(8,128)S(1)}, u32[]{:S(2)}, u32[]{:S(2)}) collective-permute-start(f32[2,64,128]{2,1,0:T(8,128)} %get-tuple-element.55), channel_id=1, source_target_pairs={{0,1},{1,0},{2,3},{3,2},{4,5},{5,4},{6,7},{7,6},{8,9},{9,8},{10,11... | collective-permute-start | bytes 196616 | tf_op jit(solution)/shard_map/ppermute | solution.py:433
  126.0 4.5 %collective-permute-start.17 = (f32[2,64,128]{2,1,0:T(8,128)}, f32[2,64,128]{2,1,0:T(8,128)S(1)}, u32[]{:S(2)}, u32[]{:S(2)}) collective-permute-start(f32[2,64,128]{2,1,0:T(8,128)} %get-tuple-element.56), channel_id=1, source_target_pairs={{0,1},{1,0},{2,3},{3,2},{4,5},{5,4},{6,7},{7,6},{8,9},{9,8},{10,11... | collective-permute-start | bytes 196616 | tf_op jit(solution)/shard_map/ppermute | solution.py:434
  130.5 0.6 copy-start.16
  131.1 0.6 copy-start.17

commit v2 on v1

--- a/solution.py
+++ b/solution.py
@@ -16,6 +16,7 @@
 ZETA = 1.149604398860241
 INVERSE_ZETA = 1.0 / 1.149604398860241
 LANES = 128
+EDGE = 8
 
 
 def for_right(s_2, d_2, s_1, d_1):
@@ -124,7 +125,7 @@
 
 
 def edges(sizes, x):
-    count = min(8, sizes.z)
+    count = min(16, sizes.z)
     out = jax.ShapeDtypeStruct((sizes.z, 2, sizes.x), jnp.float32)
     spec = pl.BlockSpec((count, 2, sizes.x), lambda i: (i, 0, 0))
     return pl.pallas_call(
@@ -180,15 +181,8 @@
 
 def across_planes(sizes, count, refs, work):
     x_ref, yb_ref, ya_ref, xb_ref, xa_ref, high_ref, low_ref, rim_ref = refs
-    n = sizes.x // 2
-    at = lax.broadcasted_iota(jnp.int32, (n, LANES), 0)
-
-    def shifted_next(v, edge):
-        return jnp.where(at == n - 1, edge, pltpu.roll(v, n - 1, 0))
-
-    def shifted_prev(v, edge):
-        return jnp.where(at == 0, edge, pltpu.roll(v, 1, 0))
-
+    nx = sizes.x
+    n = nx // 2
     for p in range(count):
         rim = jnp.concatenate([yb_ref[p], ya_ref[p]], axis=0)
         high = rim.astype(jnp.bfloat16).astype(jnp.float32)
@@ -196,89 +190,115 @@
         across = times(x_ref[p], high_ref, low_ref) + dot(packed.T.astype(jnp.bfloat16), rim_ref[...])
         for c in range(sizes.out // LANES):
             lanes = slice(c * LANES, (c + 1) * LANES)
-            work[p, c] = across[:, lanes]
-            s = work[p, c, pl.ds(0, n, stride=2), :]
-            d = work[p, c, pl.ds(1, n, stride=2), :]
-            a, b = xb_ref[p, 0:1, lanes], xb_ref[p, 1:2, lanes]
-            s_n, c_n = xa_ref[p, 0:1, lanes], xa_ref[p, 1:2, lanes]
-            d1 = d + ALPHA * (s + shifted_next(s, s_n))
-            d1_b = a + ALPHA * s[0:1]
-            s1 = s + BETA * (shifted_prev(d1, d1_b) + d1)
-            s1_b = b + BETA * d1_b
-            s1_a = c_n + BETA * d1[n - 1 : n]
-            d2 = d1 + GAMMA * (s1 + shifted_next(s1, s1_a))
-            d2_b = d1_b + GAMMA * (s1_b + s1[0:1])
-            s2 = s1 + DELTA * (shifted_prev(d2, d2_b) + d2)
-            work[p, c, pl.ds(0, n, stride=2), :] = s2 * ZETA
-            work[p, c, pl.ds(1, n, stride=2), :] = d2 * INVERSE_ZETA
+
+            def row(ref, k):
+                return ref[p, k : k + 1, lanes]
+
+            def at(start):
+                return pl.ds(EDGE + start, n, stride=2)
+
+            def one(k):
+                return slice(EDGE + k, EDGE + k + 1)
+
+            work[p, c, EDGE : EDGE + nx] = across[:, lanes]
+            work[p, c, one(nx)] = row(xa_ref, 0)
+            s = work[p, c, at(0)]
+            d1 = work[p, c, at(1)] + ALPHA * (s + work[p, c, at(2)])
+            d1_b = row(xb_ref, 0) + ALPHA * s[0:1]
+            work[p, c, at(1)] = d1
+            work[p, c, one(-1)] = d1_b
+            s1 = s + BETA * (work[p, c, at(-1)] + d1)
+            s1_b = row(xb_ref, 1) + BETA * d1_b
+            work[p, c, at(0)] = s1
+            work[p, c, one(nx)] = row(xa_ref, 1) + BETA * d1[n - 1 : n]
+            d2 = d1 + GAMMA * (s1 + work[p, c, at(2)])
+            work[p, c, at(1)] = d2
+            work[p, c, one(-1)] = d1_b + GAMMA * (s1_b + s1[0:1])
+            work[p, c, at(0)] = s1 + DELTA * (work[p, c, at(-1)] + d2)
+
+
+def x_scale(height):
+    even = lax.broadcasted_iota(jnp.int32, (height, LANES), 0) % 2 == 0
+    return jnp.where(even, ZETA, INVERSE_ZETA).astype(jnp.float32)
 
 
 def ends_kernel(sizes, *args):
-    refs, left_ref, right_ref, work = args[:8], args[8], args[9], args[10]
+    refs, out_ref, work = args[:8], args[8], args[9]
     across_planes(sizes, 4, refs, work)
     for c in range(sizes.out // LANES):
         lanes = slice(c * LANES, (c + 1) * LANES)
-        v = [work[p, c] for p in range(4)]
+        v = [work[p, c, EDGE : EDGE + sizes.x] for p in range(4)]
 
         @pl.when(pl.program_id(0) == 0)
         def _():
-            left_ref[0, :, lanes], left_ref[1, :, lanes] = for_left(*v[:3])
+            out_ref[0, :, lanes], out_ref[1, :, lanes] = for_left(*v[:3])
 
         @pl.when(pl.program_id(0) == 1)
         def _():
-            right_ref[0, :, lanes], right_ref[1, :, lanes] = for_right(*v)
-
-
-def stream_kernel(sizes, steps, more, *args):
+            out_ref[2, :, lanes], out_ref[3, :, lanes] = for_right(*v)
+
+
+def stream_kernel(sizes, group, steps, more, *args):
     refs, out_ref = args[:8], args[8]
     next_ref = args[9] if more else None
     work, state = args[-2:]
     step = pl.program_id(0)
     nx = sizes.x
     chunk = min(32, nx)
+    even_scale = x_scale(chunk) * ZETA
+    odd_scale = x_scale(chunk) * INVERSE_ZETA
+
+    def take(pairs, slot):
+        for c in range(sizes.out // LANES):
+            lanes = slice(c * LANES, (c + 1) * LANES)
+            for r in range(nx // chunk):
+                at = slice(r * chunk, (r + 1) * chunk)
+                held = slice(EDGE + r * chunk, EDGE + (r + 1) * chunk)
+                s, d, d1_b, s1_b, d2_b = (state[k, c, at] for k in range(5))
+                for q, pair in enumerate(pairs, slot):
+                    s_n, d_n = work[2 * pair, c, held], work[2 * pair + 1, c, held]
+                    d1 = d + ALPHA * (s + s_n)
+                    s1 = s + BETA * (d1_b + d1)
+                    d2 = d1_b + GAMMA * (s1_b + s1)
+                    even = (s1_b + DELTA * (d2_b + d2)) * even_scale
+                    out_ref[2 * q, at, lanes] = even
+                    out_ref[2 * q + 1, at, lanes] = d2 * odd_scale
+                    if more:
+                        work[2 * pair, c, held] = even
+                    s, d, d1_b, s1_b, d2_b = s_n, d_n, d1, s1, d2
+                for k, v in enumerate((s, d, d1_b, s1_b, d2_b)):
+                    state[k, c, at] = v
+            if more:
+                for q, pair in enumerate(pairs, slot):
+                    next_ref[q, :, lanes] = work[2 * pair, c, pl.ds(EDGE, nx // 2, stride=2), :]
+
+    late = range(2, group // 2)
 
     @pl.when(step == 0)
     def _():
         state[...] = jnp.zeros_like(state)
+        work[...] = jnp.zeros_like(work)
 
     @pl.when(step < steps)
     def _():
-        across_planes(sizes, 4, refs, work)
+        take(late, 0)
+        across_planes(sizes, group, refs, work)
 
     @pl.when(step == steps)
     def _():
-        work[...] = jnp.zeros_like(work)
-
-    for c in range(sizes.out // LANES):
-        lanes = slice(c * LANES, (c + 1) * LANES)
-        for r in range(nx // chunk):
-            at = slice(r * chunk, (r + 1) * chunk)
-            s, d, d1_b, s1_b, d2_b = (state[k, c, at] for k in range(5))
-            for q in range(2):
-                s_n, d_n = work[2 * q, c, at], work[2 * q + 1, c, at]
-                d1 = d + ALPHA * (s + s_n)
-                s1 = s + BETA * (d1_b + d1)
-                d2 = d1_b + GAMMA * (s1_b + s1)
-                even = (s1_b + DELTA * (d2_b + d2)) * ZETA
-                out_ref[2 * q, at, lanes] = even
-                out_ref[2 * q + 1, at, lanes] = d2 * INVERSE_ZETA
-                if more:
-                    work[2 * q, c, at] = even
-                s, d, d1_b, s1_b, d2_b = s_n, d_n, d1, s1, d2
-            for k, v in enumerate((s, d, d1_b, s1_b, d2_b)):
-                state[k, c, at] = v
-        if more:
-            for q in range(2):
-                next_ref[q, :, lanes] = work[2 * q, c, pl.ds(0, nx // 2, stride=2), :]
-
-
-def across_specs(sizes, place):
+        take(late, 0)
+        work[:4] = jnp.zeros((4,) + work.shape[1:], jnp.float32)
+
+    take(range(2), len(late))
+
+
+def across_specs(sizes, count, place):
     return [
-        pl.BlockSpec((4, sizes.x, sizes.lanes), place),
-        pl.BlockSpec((4, 2, sizes.x), place),
-        pl.BlockSpec((4, 2, sizes.x), place),
-        pl.BlockSpec((4, 2, sizes.out), place),
-        pl.BlockSpec((4, 2, sizes.out), place),
+        pl.BlockSpec((count, sizes.x, sizes.lanes), place),
+        pl.BlockSpec((count, 2, sizes.x), place),
+        pl.BlockSpec((count, 2, sizes.x), place),
+        pl.BlockSpec((count, 2, sizes.out), place),
+        pl.BlockSpec((count, 2, sizes.out), place),
         whole(sizes.high.shape),
         whole(sizes.low.shape),
         whole(sizes.rim_packed.shape),
@@ -294,15 +314,15 @@
 
 
 def ends(sizes, *operands):
-    out = jax.ShapeDtypeStruct((2, sizes.x, sizes.out), jnp.float32)
+    out = jax.ShapeDtypeStruct((4, sizes.x, sizes.out), jnp.float32)
     last = sizes.z // 4 - 1
     return pl.pallas_call(
         functools.partial(ends_kernel, sizes),
         grid=(2,),
-        in_specs=across_specs(sizes, lambda i: (i * last, 0, 0)),
-        out_specs=[whole(out.shape), whole(out.shape)],
-        out_shape=[out, out],
-        scratch_shapes=[pltpu.VMEM((4, sizes.out // LANES, sizes.x, LANES), jnp.float32)],
+        in_specs=across_specs(sizes, 4, lambda i: (i * last, 0, 0)),
+        out_specs=whole(out.shape),
+        out_shape=out,
+        scratch_shapes=[pltpu.VMEM((4, sizes.out // LANES, sizes.x + 2 * EDGE, LANES), jnp.float32)],
         cost_estimate=cost(sizes, 8),
         name="ends",
     )(*operands, sizes.high, sizes.low, sizes.rim_packed)
@@ -310,21 +330,22 @@
 
 def stream(sizes, more, *operands):
     z, nx, width = sizes.z, sizes.x, sizes.out
-    steps = z // 4
+    group = min(8, z)
+    steps = z // group
     behind = lambda i: (jnp.maximum(i - 1, 0), 0, 0)
     out_shape = [jax.ShapeDtypeStruct((z, nx, width), jnp.float32)]
-    out_specs = [pl.BlockSpec((4, nx, width), behind)]
+    out_specs = [pl.BlockSpec((group, nx, width), behind)]
     if more:
         out_shape.append(jax.ShapeDtypeStruct((z // 2, nx // 2, width), jnp.float32))
-        out_specs.append(pl.BlockSpec((2, nx // 2, width), behind))
+        out_specs.append(pl.BlockSpec((group // 2, nx // 2, width), behind))
     return pl.pallas_call(
-        functools.partial(stream_kernel, sizes, steps, more),
+        functools.partial(stream_kernel, sizes, group, steps, more),
         grid=(steps + 1,),
-        in_specs=across_specs(sizes, lambda i: (jnp.minimum(i, steps - 1), 0, 0)),
+        in_specs=across_specs(sizes, group, lambda i: (jnp.minimum(i, steps - 1), 0, 0)),
         out_specs=out_specs,
         out_shape=out_shape,
         scratch_shapes=[
-            pltpu.VMEM((4, width // LANES, nx, LANES), jnp.float32),
+            pltpu.VMEM((group, width // LANES, nx + 2 * EDGE, LANES), jnp.float32),
             pltpu.VMEM((5, width // LANES, nx, LANES), jnp.float32),
         ],
         cost_estimate=cost(sizes, z),
@@ -332,7 +353,7 @@
     )(*operands, sizes.high, sizes.low, sizes.rim_packed)
 
 
-def finish_kernel(sizes, more, zb_ref, za_ref, t_ref, *rest):
+def finish_kernel(sizes, more, z_ref, t_ref, *rest):
     if more:
         _, out_ref, next_ref, work = rest
     else:
@@ -340,17 +361,18 @@
     nx = sizes.x
     rim = lifting_matrices(sizes.z)[1]
     single = sizes.z == 4
+    scale = x_scale(nx)
 
     def apply(sides):
         for k in range(4):
             for c in range(sizes.out // LANES):
                 lanes = slice(c * LANES, (c + 1) * LANES)
-                total = t_ref[k, :, lanes]
+                total = jnp.zeros((nx, LANES), jnp.float32)
                 for h in range(4):
                     factor = rim[h, k if h < 2 else sizes.z - 4 + k]
                     if factor != 0.0 and h // 2 in sides:
-                        ref = (zb_ref, za_ref)[h // 2]
-                        total = total + float(factor) * ref[h % 2, :, lanes]
+                        total = total + float(factor) * z_ref[(h + 2) % 4, :, lanes]
+                total = t_ref[k, :, lanes] + scale * total
                 out_ref[k, :, lanes] = total
                 if more and k % 2 == 0:
                     work[c] = total
@@ -363,7 +385,7 @@
         pl.when(pl.program_id(0) == 1)(lambda: apply((1,)))
 
 
-def finish(sizes, made, z_before, z_after):
+def finish(sizes, made, z_planes):
     more = len(made) == 2
     z, nx, width = sizes.z, sizes.x, sizes.out
     last = z // 4 - 1
@@ -376,39 +398,55 @@
     return pl.pallas_call(
         functools.partial(finish_kernel, sizes, more),
         grid=(min(2, last + 1),),
-        in_specs=[whole((2, nx, width)), whole((2, nx, width))] + specs,
+        in_specs=[whole((4, nx, width))] + specs,
         out_specs=specs,
         out_shape=[jax.ShapeDtypeStruct(m.shape, m.dtype) for m in made],
-        input_output_aliases={2 + k: k for k in range(len(made))},
+        input_output_aliases={1 + k: k for k in range(len(made))},
         scratch_shapes=scratch,
         name="finish",
-    )(z_before, z_after, *made)
-
-
-def place_kernel(count, t_ref, r_ref, spread_ref, out_ref, work):
-    nx, width = t_ref.shape[2], t_ref.shape[3]
+    )(z_planes, *made)
+
+
+def spread_lanes(rows, table):
+    high = rows.astype(jnp.bfloat16)
+    middle, low = halves(rows - high.astype(jnp.float32))
+    return dot(high, table) + dot(middle, table) + dot(low, table)
+
+
+def put_inner(plane, inner, table, work):
+    nx, width = plane.shape
     n = nx // 2
     even_lane = lax.broadcasted_iota(jnp.int32, (n, LANES), 1) % 2 == 0
+    spread = spread_lanes(inner, table)
+    for c in range(width // LANES):
+        lanes = slice(c * LANES, (c + 1) * LANES)
+        work[c] = plane[:, lanes]
+        even_rows = work[c, pl.ds(0, n, stride=2), :]
+        work[c, pl.ds(0, n, stride=2), :] = jnp.where(even_lane, spread[:, lanes], even_rows)
+
+
+def place_kernel(count, t_ref, middle_ref, inner_ref, outer_table_ref, inner_table_ref, out_ref, work, inner_work):
+    width, middle_width = t_ref.shape[3], middle_ref.shape[2]
     for p in range(count):
-        rest = r_ref[p]
-        high = rest.astype(jnp.bfloat16)
-        rest = rest - high.astype(jnp.float32)
-        middle, low = halves(rest)
-        table = spread_ref[...]
-        spread = dot(high, table) + dot(middle, table) + dot(low, table)
+        middle = middle_ref[p]
+        if p % 2 == 0:
+            put_inner(middle, inner_ref[p // 2], inner_table_ref[...], inner_work)
+            middle = jnp.concatenate([inner_work[c] for c in range(middle_width // LANES)], axis=1)
+        put_inner(t_ref[p, 0], middle, outer_table_ref[...], work)
         for c in range(width // LANES):
-            lanes = slice(c * LANES, (c + 1) * LANES)
-            work[c] = t_ref[p, 0, :, lanes]
-            even_rows = work[c, pl.ds(0, n, stride=2), :]
-            work[c, pl.ds(0, n, stride=2), :] = jnp.where(even_lane, spread[:, lanes], even_rows)
-            out_ref[p, 0, :, lanes] = work[c]
-
-
-def place(t, r):
+            out_ref[p, 0, :, c * LANES : (c + 1) * LANES] = work[c]
+
+
+def spread_table(inner, outer):
+    table = np.zeros((inner, outer), np.float32)
+    for j in range(min(inner, outer // 2)):
+        table[j, 2 * j] = 1.0
+    return table.astype(jnp.bfloat16)
+
+
+def place(t, middle, inner):
     z, nx, width = t.shape
-    table = np.zeros((r.shape[2], width), np.float32)
-    for j in range(min(r.shape[2], width // 2)):
-        table[j, 2 * j] = 1.0
+    tables = spread_table(middle.shape[2], width), spread_table(inner.shape[2], middle.shape[2])
     count = min(8, z // 2)
     spec = pl.BlockSpec((count, 1, nx, width), lambda i: (i, 0, 0, 0))
     paired = t.reshape(z // 2, 2, nx, width)
@@ -417,15 +455,20 @@
         grid=(z // 2 // count,),
         in_specs=[
             spec,
-            pl.BlockSpec((count,) + r.shape[1:], lambda i: (i, 0, 0)),
-            whole(table.shape),
+            pl.BlockSpec((count,) + middle.shape[1:], lambda i: (i, 0, 0)),
+            pl.BlockSpec((count // 2,) + inner.shape[1:], lambda i: (i, 0, 0)),
+            whole(tables[0].shape),
+            whole(tables[1].shape),
         ],
         out_specs=spec,
         out_shape=jax.ShapeDtypeStruct(paired.shape, jnp.float32),
         input_output_aliases={0: 0},
-        scratch_shapes=[pltpu.VMEM((width // LANES, nx, LANES), jnp.float32)],
+        scratch_shapes=[
+            pltpu.VMEM((width // LANES, nx, LANES), jnp.float32),
+            pltpu.VMEM((middle.shape[2] // LANES,) + middle.shape[1:2] + (LANES,), jnp.float32),
+        ],
         name="place",
-    )(paired, r, table.astype(jnp.bfloat16)).reshape(t.shape)
+    )(paired, middle, inner, *tables).reshape(t.shape)
 
 
 def exchange(axis, left, right):
@@ -435,14 +478,22 @@
     return before, after
 
 
+def exchange_z(planes):
+    count = lax.axis_size("gz")
+    if count == 2:
+        return lax.ppermute(planes, "gz", [(0, 1), (1, 0)])
+    before, after = exchange("gz", planes[:2], planes[2:])
+    return jnp.concatenate([after, before])
+
+
 def level(sizes, x, more):
     y_before, y_after = exchange("gy", *edges(sizes, x))
     rim = jnp.concatenate([y_before, y_after], axis=1)
     rim_rows = jnp.concatenate([rim[:, :, :8], rim[:, :, -8:]], axis=2).swapaxes(1, 2)
     x_before, x_after = exchange("gx", *rows(sizes, x, rim_rows))
-    sides = (y_before, y_after, x_before, x_after)
-    z_before, z_after = exchange("gz", *ends(sizes, x, *sides))
-    return finish(sizes, stream(sizes, more, x, *sides), z_before, z_after)
+    operands = (x, y_before, y_after, x_before, x_after)
+    z_planes = exchange_z(ends(sizes, *operands))
+    return finish(sizes, stream(sizes, more, *operands), z_planes)
 
 
 def local(turbulence):
@@ -455,10 +506,7 @@
         done.append(made[0])
         if more:
             current, step, valid = made[1], 2, valid // 2
-    result = done[-1]
-    for finer in reversed(done[:-1]):
-        result = place(finer, result)
-    return result[:, :, : turbulence.shape[2]]
+    return place(*done)[:, :, : turbulence.shape[2]]
 
 
 def solution(mesh):

time: 146 us -> 134 us (0.918)
  Pallas kernels: 92.2 us -> 82.5 us
  starting transfers between devices: 23.5 us -> 20.1 us
  waiting for transfers between devices: 19.1 us -> 22.1 us
    pallas_call x3, Pallas kernels: 41 us -> 35.1 us  [stream(): pl.pallas_call(functools.partial(stream_kernel, sizes, group, steps, more...]
    ppermute x9 -> x6, starting transfers between devices: 7.63 us -> 3.07 us  [exchange(): lax.ppermute(right, axis, [(i, (i + 1) % count) for i in range(count)])]
    ppermute x0 -> x3, waiting for transfers between devices: none -> 3 us  [exchange_z(): return lax.ppermute(planes, 'gz', [(0, 1), (1, 0)])]
    pallas_call x3, Pallas kernels: 15.6 us -> 12.9 us  [edges(): pl.pallas_call(functools.partial(edges_kernel, sizes, count), grid=(sizes...]
    ppermute x0 -> x3, starting transfers between devices: none -> 2.67 us  [exchange_z(): return lax.ppermute(planes, 'gz', [(0, 1), (1, 0)])]
    ppermute x9 -> x6, starting transfers between devices: 15.9 us -> 14.3 us  [exchange(): lax.ppermute(left, axis, [(i, (i - 1) % count) for i in range(count)])]
    pallas_call x2 -> x1, Pallas kernels: 11.2 us -> 10.1 us  [place(): pl.pallas_call(functools.partial(place_kernel, count), grid=(z // 2 // co...]
    unnamed x36 -> x30, local copies, waits for them, and re-layouts: 5.97 us -> 5.39 us
  transfers between devices with their start and end apart: 18 -> 15, of which waited for: 9 -> 11; matrix products, arithmetic and copies ran while one was open for 0% -> 0% of each run, Pallas kernels for 28% -> 26%
where the time goes in v2:
time: 134 us
  Pallas kernels  82.5 us (62%)
  waiting for transfers between devices  22.1 us (16%)
  starting transfers between devices  20.1 us (15%)
  local copies, waits for them, and re-layouts  8.42 us (6%)
    pallas_call x3, Pallas kernels, stream(): pl.pallas_call(functools.partial(stream_kernel, sizes, group, steps, more...  35.1 us
    ppermute x6, waiting for transfers between devices, exchange(): lax.ppermute(right, axis, [(i, (i + 1) % count) for i in range(count)])  15.1 us
    ppermute x6, starting transfers between devices, exchange(): lax.ppermute(left, axis, [(i, (i - 1) % count) for i in range(count)])  14.3 us
    pallas_call x3, Pallas kernels, edges(): pl.pallas_call(functools.partial(edges_kernel, sizes, count), grid=(sizes...  12.9 us
    pallas_call x1, Pallas kernels, place(): pl.pallas_call(functools.partial(place_kernel, count), grid=(z // 2 // co...  10.1 us
    pallas_call x3, Pallas kernels, ends(): pl.pallas_call(functools.partial(ends_kernel, sizes), grid=(2,), in_specs...  9.93 us
    pallas_call x3, Pallas kernels, rows(): pl.pallas_call(functools.partial(rows_kernel, sizes), grid=(1,), in_specs...  7.31 us
    pallas_call x3, Pallas kernels, finish(): pl.pallas_call(functools.partial(finish_kernel, sizes, more), grid=(min(2...  7.07 us
  transfers between devices with their start and end apart: 15, of which 11 were waited for; matrix products, arithmetic and copies ran while one was open for 0% of the time, Pallas kernels for 26%

profile of v2, /device:TPU:0, one launch (start us, length us, event | category | flops | bytes accessed | tf_op | source)
XLA Modules:
  0.0 133.7 jit_solution(254249234240532049)
XLA Ops:
  0.0 7.8 %edges.3 = (f32[64,2,256]{2,1,0:T(2,128)}, f32[64,2,256]{2,1,0:T(2,128)}) custom-call(f32[64,256,256]{2,1,0:T(8,128)} %args_0_.6), custom_call_target="tpu_custom_call" | custom-call | tf_op jit(solution)/shard_map/edges/pallas_call | solution.py:131
  7.8 0.5 collective-permute-start
  8.3 1.9 %collective-permute-start.1 = (f32[64,2,256]{2,1,0:T(2,128)}, f32[64,2,256]{2,1,0:T(2,128)S(1)}, u32[]{:S(2)}, u32[]{:S(2)}) collective-permute-start(f32[64,2,256]{2,1,0:T(2,128)} %get-tuple-element.26), channel_id=1, source_target_pairs={{0,6},{2,0},{4,2},{6,4},{1,7},{3,1},{5,3},{7,5},{8,14},{10,8},{12,... | collective-permute-start | bytes 393224 | tf_op jit(solution)/shard_map/ppermute | solution.py:477
  10.2 2.9 %collective-permute-done.args_1_ = f32[64,2,256]{2,1,0:T(2,128)S(1)} collective-permute-done((f32[64,2,256]{2,1,0:T(2,128)}, f32[64,2,256]{2,1,0:T(2,128)S(1)}, u32[]{:S(2)}, u32[]{:S(2)}) %collective-permute-start) | collective-permute-done | bytes 131104 | tf_op jit(solution)/shard_map/ppermute | solution.py:476
  13.0 1.3 collective-permute-done.1.args_2_
  14.6 1.2 copy.30.rim_rows_ref
  15.9 3.3 %rows.3 = (f32[64,2,256]{2,1,0:T(2,128)}, f32[64,2,256]{2,1,0:T(2,128)}) custom-call(f32[64,256,256]{2,1,0:T(8,128)} %args_0_.6, f32[64,256,256]{2,1,0:T(8,128)} %args_0_.6, f32[64,16,4]{2,1,0:T(8,128)} %copy.30.rim_rows_ref, bf16[256,256]{1,0:T(8,128)(2,1)} %constant.28.clone.high_ref.args_5_, bf16[256,256]{1,0:T(8,128)(2,1)} %constant.29.clone.low_ref.args_6_, ...), custom_call_target="tpu_custom_call" | custom-call | tf_op jit(solution)/shard_map/rows/pallas_call | solution.py:165
  19.2 1.6 %collective-permute-start.2 = (f32[64,2,256]{2,1,0:T(2,128)}, f32[64,2,256]{2,1,0:T(2,128)S(1)}, u32[]{:S(2)}, u32[]{:S(2)}) collective-permute-start(f32[64,2,256]{2,1,0:T(2,128)} %get-tuple-element.27), channel_id=1, source_target_pairs={{0,8},{8,16},{16,24},{24,0},{1,9},{9,17},{17,25},{25,1},{2,10},{10... | collective-permute-start | bytes 393224 | tf_op jit(solution)/shard_map/ppermute | solution.py:476
  20.8 2.2 %collective-permute-start.3 = (f32[64,2,256]{2,1,0:T(2,128)}, f32[64,2,256]{2,1,0:T(2,128)S(1)}, u32[]{:S(2)}, u32[]{:S(2)}) collective-permute-start(f32[64,2,256]{2,1,0:T(2,128)} %get-tuple-element.28), channel_id=1, source_target_pairs={{0,24},{8,0},{16,8},{24,16},{1,25},{9,1},{17,9},{25,17},{2,26},{10... | collective-permute-start | bytes 393224 | tf_op jit(solution)/shard_map/ppermute | solution.py:477
  23.0 4.5 %collective-permute-done.2.args_3_ = f32[64,2,256]{2,1,0:T(2,128)S(1)} collective-permute-done((f32[64,2,256]{2,1,0:T(2,128)}, f32[64,2,256]{2,1,0:T(2,128)S(1)}, u32[]{:S(2)}, u32[]{:S(2)}) %collective-permute-start.2) | collective-permute-done | bytes 131104 | tf_op jit(solution)/shard_map/ppermute | solution.py:476
  27.5 2.5 %collective-permute-done.3.args_4_ = f32[64,2,256]{2,1,0:T(2,128)S(1)} collective-permute-done((f32[64,2,256]{2,1,0:T(2,128)}, f32[64,2,256]{2,1,0:T(2,128)S(1)}, u32[]{:S(2)}, u32[]{:S(2)}) %collective-permute-start.3) | collective-permute-done | bytes 131104 | tf_op jit(solution)/shard_map/ppermute | solution.py:477
  30.0 0.6 copy-done.9
  30.7 4.7 %ends.3 = f32[4,256,256]{2,1,0:T(8,128)} custom-call(f32[64,256,256]{2,1,0:T(8,128)} %args_0_.6, f32[64,2,256]{2,1,0:T(2,128)} %copy-done, f32[64,2,256]{2,1,0:T(2,128)} %copy-done.1, f32[64,2,256]{2,1,0:T(2,128)} %copy-done.8, f32[64,2,256]{2,1,0:T(2,128)} %copy-done.9, bf16[256,256]{1,0:T(8,128)(2,1)} %constant.28.clone.high_ref.args_5_, ...), custom_call_target="tpu_custom_call" | custom-call | flops 1073741824 | bytes 4194304 | tf_op jit(solution)/shard_map/ends/pallas_call | solution.py:319
  35.4 1.5 %collective-permute-start.4 = (f32[4,256,256]{2,1,0:T(8,128)}, f32[4,256,256]{2,1,0:T(8,128)S(1)}, u32[]{:S(2)}, u32[]{:S(2)}) collective-permute-start(f32[4,256,256]{2,1,0:T(8,128)} %ends.3), channel_id=1, source_target_pairs={{0,1},{1,0},{2,3},{3,2},{4,5},{5,4},{6,7},{7,6},{8,9},{9,8},{10,11... | collective-permute-start | bytes 3145736 | tf_op jit(solution)/shard_map/ppermute | solution.py:484
  36.9 25.1 %stream.3 = (f32[64,256,256]{2,1,0:T(8,128)}, f32[32,128,256]{2,1,0:T(8,128)}) custom-call(f32[64,256,256]{2,1,0:T(8,128)} %args_0_.6, f32[64,2,256]{2,1,0:T(2,128)} %copy-done, f32[64,2,256]{2,1,0:T(2,128)} %copy-done.1, f32[64,2,256]{2,1,0:T(2,128)} %copy-done.8, f32[64,2,256]{2,1,0:T(2,128)} %copy-done.9, ...), custom_call_target="tpu_custom_call" | custom-call | flops 8589934592 | bytes 33554432 | tf_op jit(solution)/shard_map/stream/pallas_call | solution.py:341
  62.1 1.0 copy-done.2
  63.1 3.4 %finish.3 = (f32[64,256,256]{2,1,0:T(8,128)}, f32[32,128,256]{2,1,0:T(8,128)}) custom-call(f32[4,256,256]{2,1,0:T(8,128)} %copy-done.2, f32[64,256,256]{2,1,0:T(8,128)} %get-tuple-element.29.t_ref, f32[32,128,256]{2,1,0:T(8,128)} %get-tuple-element.30.rest_0_), custom_call_target="tpu_custom_call", output_to_operand_aliasing={{0}: (1, {}), {1}: (2, {})} | custom-call | tf_op jit(solution)/shard_map/finish/pallas_call | solution.py:398
  66.4 3.2 %edges.4 = (f32[32,2,128]{2,1,0:T(2,128)}, f32[32,2,128]{2,1,0:T(2,128)}) custom-call(f32[32,128,256]{2,1,0:T(8,128)} %get-tuple-element.32.x_ref.top_ref.bottom_ref.args_0_), custom_call_target="tpu_custom_call" | custom-call | tf_op jit(solution)/shard_map/edges/pallas_call | solution.py:131
  69.6 1.7 %collective-permute-start.6 = (f32[32,2,128]{2,1,0:T(2,128)}, f32[32,2,128]{2,1,0:T(2,128)S(1)}, u32[]{:S(2)}, u32[]{:S(2)}) collective-permute-start(f32[32,2,128]{2,1,0:T(2,128)} %get-tuple-element.34), channel_id=1, source_target_pairs={{0,6},{2,0},{4,2},{6,4},{1,7},{3,1},{5,3},{7,5},{8,14},{10,8},{12,... | collective-permute-start | bytes 98312 | tf_op jit(solution)/shard_map/ppermute | solution.py:477
  71.4 1.8 %collective-permute-done.5.args_1_ = f32[32,2,128]{2,1,0:T(2,128)S(1)} collective-permute-done((f32[32,2,128]{2,1,0:T(2,128)}, f32[32,2,128]{2,1,0:T(2,128)S(1)}, u32[]{:S(2)}, u32[]{:S(2)}) %collective-permute-start.5) | collective-permute-done | bytes 32800 | tf_op jit(solution)/shard_map/ppermute | solution.py:476
  73.5 1.0 copy.31.rim_rows_ref
  74.4 2.2 %rows.4 = (f32[32,2,128]{2,1,0:T(2,128)}, f32[32,2,128]{2,1,0:T(2,128)}) custom-call(f32[32,128,256]{2,1,0:T(8,128)} %get-tuple-element.32.x_ref.top_ref.bottom_ref.args_0_, f32[32,128,256]{2,1,0:T(8,128)} %get-tuple-element.32.x_ref.top_ref.bottom_ref.args_0_, f32[32,16,4]{2,1,0:T(8,128)} %copy.31.rim_rows_ref, ...), custom_call_target="tpu_custom_call" | custom-call | tf_op jit(solution)/shard_map/rows/pallas_call | solution.py:165
  76.6 0.9 collective-permute-start.7
  77.6 2.9 %collective-permute-start.8 = (f32[32,2,128]{2,1,0:T(2,128)}, f32[32,2,128]{2,1,0:T(2,128)S(1)}, u32[]{:S(2)}, u32[]{:S(2)}) collective-permute-start(f32[32,2,128]{2,1,0:T(2,128)} %get-tuple-element.36), channel_id=1, source_target_pairs={{0,24},{8,0},{16,8},{24,16},{1,25},{9,1},{17,9},{25,17},{2,26},{10... | collective-permute-start | bytes 98312 | tf_op jit(solution)/shard_map/ppermute | solution.py:477
  80.4 2.4 %collective-permute-done.7.args_3_ = f32[32,2,128]{2,1,0:T(2,128)S(1)} collective-permute-done((f32[32,2,128]{2,1,0:T(2,128)}, f32[32,2,128]{2,1,0:T(2,128)S(1)}, u32[]{:S(2)}, u32[]{:S(2)}) %collective-permute-start.7) | collective-permute-done | bytes 32800 | tf_op jit(solution)/shard_map/ppermute | solution.py:476
  82.8 0.6 copy-done.10
  83.4 0.6 copy-done.11
  84.0 2.9 %ends.4 = f32[4,128,128]{2,1,0:T(8,128)} custom-call(f32[32,128,256]{2,1,0:T(8,128)} %get-tuple-element.32.x_ref.top_ref.bottom_ref.args_0_, f32[32,2,128]{2,1,0:T(2,128)} %copy-done.3, f32[32,2,128]{2,1,0:T(2,128)} %copy-done.4, f32[32,2,128]{2,1,0:T(2,128)} %copy-done.10, f32[32,2,128]{2,1,0:T(2,128)} %copy-done.11, ...), custom_call_target="tpu_custom_call" | custom-call | flops 268435456 | bytes 1572864 | tf_op jit(solution)/shard_map/ends/pallas_call | solution.py:319
  87.4 7.0 %stream.4 = (f32[32,128,128]{2,1,0:T(8,128)}, f32[16,64,128]{2,1,0:T(8,128)}) custom-call(f32[32,128,256]{2,1,0:T(8,128)} %get-tuple-element.32.x_ref.top_ref.bottom_ref.args_0_, f32[32,2,128]{2,1,0:T(2,128)} %copy-done.3, f32[32,2,128]{2,1,0:T(2,128)} %copy-done.4, f32[32,2,128]{2,1,0:T(2,128)} %copy-done.10, f32[32,2,128]{2,1,0:T(2,128)} %copy-done.11, ...), custom_call_target="tpu_custom_call" | custom-call | flops 1073741824 | bytes 6291456 | tf_op jit(solution)/shard_map/stream/pallas_call | solution.py:341
  94.5 0.9 collective-permute-done.9.z_ref
  95.4 0.7 copy-done.7
  96.1 2.0 %finish.4 = (f32[32,128,128]{2,1,0:T(8,128)}, f32[16,64,128]{2,1,0:T(8,128)}) custom-call(f32[4,128,128]{2,1,0:T(8,128)} %copy-done.7, f32[32,128,128]{2,1,0:T(8,128)} %get-tuple-element.37.t_ref, f32[16,64,128]{2,1,0:T(8,128)} %get-tuple-element.38.rest_0_), custom_call_target="tpu_custom_call", output_to_operand_aliasing={{0}: (1, {}), {1}: (2, {})} | custom-call | tf_op jit(solution)/shard_map/finish/pallas_call | solution.py:398
  98.1 2.0 %edges.5 = (f32[16,2,64]{2,1,0:T(2,128)}, f32[16,2,64]{2,1,0:T(2,128)}) custom-call(f32[16,64,128]{2,1,0:T(8,128)} %get-tuple-element.40.x_ref.top_ref.bottom_ref.args_0_), custom_call_target="tpu_custom_call" | custom-call | tf_op jit(solution)/shard_map/edges/pallas_call | solution.py:131
  100.1 1.7 %collective-permute-start.11 = (f32[16,2,64]{2,1,0:T(2,128)}, f32[16,2,64]{2,1,0:T(2,128)S(1)}, u32[]{:S(2)}, u32[]{:S(2)}) collective-permute-start(f32[16,2,64]{2,1,0:T(2,128)} %get-tuple-element.42), channel_id=1, source_target_pairs={{0,6},{2,0},{4,2},{6,4},{1,7},{3,1},{5,3},{7,5},{8,14},{10,8},{12,... | collective-permute-start | bytes 24584 | tf_op jit(solution)/shard_map/ppermute | solution.py:477
  101.8 1.6 %collective-permute-done.10.args_1_ = f32[16,2,64]{2,1,0:T(2,128)S(1)} collective-permute-done((f32[16,2,64]{2,1,0:T(2,128)}, f32[16,2,64]{2,1,0:T(2,128)S(1)}, u32[]{:S(2)}, u32[]{:S(2)}) %collective-permute-start.10) | collective-permute-done | bytes 8224 | tf_op jit(solution)/shard_map/ppermute | solution.py:476
  103.6 0.8 copy.32.rim_rows_ref
  104.4 1.9 %rows.5 = (f32[16,2,128]{2,1,0:T(2,128)}, f32[16,2,128]{2,1,0:T(2,128)}) custom-call(f32[16,64,128]{2,1,0:T(8,128)} %get-tuple-element.40.x_ref.top_ref.bottom_ref.args_0_, f32[16,64,128]{2,1,0:T(8,128)} %get-tuple-element.40.x_ref.top_ref.bottom_ref.args_0_, f32[16,16,4]{2,1,0:T(8,128)} %copy.32.rim_rows_ref, ...), custom_call_target="tpu_custom_call" | custom-call | tf_op jit(solution)/shard_map/rows/pallas_call | solution.py:165
  106.3 3.8 %collective-permute-start.13 = (f32[16,2,128]{2,1,0:T(2,128)}, f32[16,2,128]{2,1,0:T(2,128)S(1)}, u32[]{:S(2)}, u32[]{:S(2)}) collective-permute-start(f32[16,2,128]{2,1,0:T(2,128)} %get-tuple-element.44), channel_id=1, source_target_pairs={{0,24},{8,0},{16,8},{24,16},{1,25},{9,1},{17,9},{25,17},{2,26},{10... | collective-permute-start | bytes 49160 | tf_op jit(solution)/shard_map/ppermute | solution.py:477
  110.1 2.0 %collective-permute-done.12.args_3_ = f32[16,2,128]{2,1,0:T(2,128)S(1)} collective-permute-done((f32[16,2,128]{2,1,0:T(2,128)}, f32[16,2,128]{2,1,0:T(2,128)S(1)}, u32[]{:S(2)}, u32[]{:S(2)}) %collective-permute-start.12) | collective-permute-done | bytes 16416 | tf_op jit(solution)/shard_map/ppermute | solution.py:476
  112.1 0.6 copy-done.13
  112.7 0.6 copy-done.14
  113.3 2.3 %ends.5 = f32[4,64,128]{2,1,0:T(8,128)} custom-call(f32[16,64,128]{2,1,0:T(8,128)} %get-tuple-element.40.x_ref.top_ref.bottom_ref.args_0_, f32[16,2,64]{2,1,0:T(2,128)} %copy-done.5, f32[16,2,64]{2,1,0:T(2,128)} %copy-done.6, f32[16,2,128]{2,1,0:T(2,128)} %copy-done.13, f32[16,2,128]{2,1,0:T(2,128)} %copy-done.14, ...), custom_call_target="tpu_custom_call" | custom-call | flops 67108864 | bytes 524288 | tf_op jit(solution)/shard_map/ends/pallas_call | solution.py:319
  115.6 0.7 collective-permute-start.14
  116.2 3.0 %stream.5.t_ref = f32[16,64,128]{2,1,0:T(8,128)} custom-call(f32[16,64,128]{2,1,0:T(8,128)} %get-tuple-element.40.x_ref.top_ref.bottom_ref.args_0_, f32[16,2,64]{2,1,0:T(2,128)} %copy-done.5, f32[16,2,64]{2,1,0:T(2,128)} %copy-done.6, f32[16,2,128]{2,1,0:T(2,128)} %copy-done.13, f32[16,2,128]{2,1,0:T(2,128)} %copy-done.14, ...), custom_call_target="tpu_custom_call" | custom-call | flops 134217728 | bytes 1048576 | tf_op jit(solution)/shard_map/stream/pallas_call | solution.py:341
  119.2 2.1 %collective-permute-done.14.z_ref = f32[4,64,128]{2,1,0:T(8,128)S(1)} collective-permute-done((f32[4,64,128]{2,1,0:T(8,128)}, f32[4,64,128]{2,1,0:T(8,128)S(1)}, u32[]{:S(2)}, u32[]{:S(2)}) %collective-permute-start.14) | collective-permute-done | bytes 131104 | tf_op jit(solution)/shard_map/ppermute | solution.py:484
  121.2 0.7 copy-done.12
  121.9 1.7 %finish.5.inner_ref = f32[16,64,128]{2,1,0:T(8,128)} custom-call(f32[4,64,128]{2,1,0:T(8,128)} %copy-done.12, f32[16,64,128]{2,1,0:T(8,128)} %stream.5.t_ref), custom_call_target="tpu_custom_call", output_to_operand_aliasing={{}: (1, {})} | custom-call | tf_op jit(solution)/shard_map/finish/pallas_call | solution.py:398
  123.6 10.1 %place.1 = f32[32,2,256,256]{3,2,1,0:T(8,128)} custom-call(f32[32,2,256,256]{3,2,1,0:T(8,128)} %bitcast.8, f32[32,128,128]{2,1,0:T(8,128)} %get-tuple-element.39.middle_ref, f32[16,64,128]{2,1,0:T(8,128)} %finish.5.inner_ref, bf16[128,256]{1,0:T(8,128)(2,1)} %constant.40.clone.outer_table_ref, ...), custom_call_target="tpu_custom_call", output_to_operand_aliasing={{}: (0, {})} | custom-call | tf_op jit(solution)/shard_map/place/pallas_call | solution.py:453
  (37 shorter events, 1.2 us)
Async XLA Ops:
  7.8 5.3 %collective-permute-start = (f32[64,2,256]{2,1,0:T(2,128)}, f32[64,2,256]{2,1,0:T(2,128)S(1)}, u32[]{:S(2)}, u32[]{:S(2)}) collective-permute-start(f32[64,2,256]{2,1,0:T(2,128)} %get-tuple-element.25), channel_id=1, source_target_pairs={{0,2},{2,4},{4,6},{6,0},{1,3},{3,5},{5,7},{7,1},{8,10},{10,12},{12... | collective-permute-start | bytes 393224 | tf_op jit(solution)/shard_map/ppermute | solution.py:476
  8.3 6.1 %collective-permute-start.1 = (f32[64,2,256]{2,1,0:T(2,128)}, f32[64,2,256]{2,1,0:T(2,128)S(1)}, u32[]{:S(2)}, u32[]{:S(2)}) collective-permute-start(f32[64,2,256]{2,1,0:T(2,128)} %get-tuple-element.26), channel_id=1, source_target_pairs={{0,6},{2,0},{4,2},{6,4},{1,7},{3,1},{5,3},{7,5},{8,14},{10,8},{12,... | collective-permute-start | bytes 393224 | tf_op jit(solution)/shard_map/ppermute | solution.py:477
  13.0 6.1 %copy-start = (f32[64,2,256]{2,1,0:T(2,128)}, f32[64,2,256]{2,1,0:T(2,128)S(1)}, u32[]{:S(2)}) copy-start(f32[64,2,256]{2,1,0:T(2,128)S(1)} %collective-permute-done.args_1_) | copy-start | bytes 393220
  14.4 4.8 %copy-start.1 = (f32[64,2,256]{2,1,0:T(2,128)}, f32[64,2,256]{2,1,0:T(2,128)S(1)}, u32[]{:S(2)}) copy-start(f32[64,2,256]{2,1,0:T(2,128)S(1)} %collective-permute-done.1.args_2_) | copy-start | bytes 393220
  19.2 8.3 %collective-permute-start.2 = (f32[64,2,256]{2,1,0:T(2,128)}, f32[64,2,256]{2,1,0:T(2,128)S(1)}, u32[]{:S(2)}, u32[]{:S(2)}) collective-permute-start(f32[64,2,256]{2,1,0:T(2,128)} %get-tuple-element.27), channel_id=1, source_target_pairs={{0,8},{8,16},{16,24},{24,0},{1,9},{9,17},{17,25},{25,1},{2,10},{10... | collective-permute-start | bytes 393224 | tf_op jit(solution)/shard_map/ppermute | solution.py:476
  20.8 9.2 %collective-permute-start.3 = (f32[64,2,256]{2,1,0:T(2,128)}, f32[64,2,256]{2,1,0:T(2,128)S(1)}, u32[]{:S(2)}, u32[]{:S(2)}) collective-permute-start(f32[64,2,256]{2,1,0:T(2,128)} %get-tuple-element.28), channel_id=1, source_target_pairs={{0,24},{8,0},{16,8},{24,16},{1,25},{9,1},{17,9},{25,17},{2,26},{10... | collective-permute-start | bytes 393224 | tf_op jit(solution)/shard_map/ppermute | solution.py:477
  27.5 2.5 %copy-start.8 = (f32[64,2,256]{2,1,0:T(2,128)}, f32[64,2,256]{2,1,0:T(2,128)S(1)}, u32[]{:S(2)}) copy-start(f32[64,2,256]{2,1,0:T(2,128)S(1)} %collective-permute-done.2.args_3_) | copy-start | bytes 393220
  30.0 0.6 copy-start.9
  35.4 26.6 %collective-permute-start.4 = (f32[4,256,256]{2,1,0:T(8,128)}, f32[4,256,256]{2,1,0:T(8,128)S(1)}, u32[]{:S(2)}, u32[]{:S(2)}) collective-permute-start(f32[4,256,256]{2,1,0:T(8,128)} %ends.3), channel_id=1, source_target_pairs={{0,1},{1,0},{2,3},{3,2},{4,5},{5,4},{6,7},{7,6},{8,9},{9,8},{10,11... | collective-permute-start | bytes 3145736 | tf_op jit(solution)/shard_map/ppermute | solution.py:484
  62.0 1.0 copy-start.2
  69.6 3.6 %collective-permute-start.5 = (f32[32,2,128]{2,1,0:T(2,128)}, f32[32,2,128]{2,1,0:T(2,128)S(1)}, u32[]{:S(2)}, u32[]{:S(2)}) collective-permute-start(f32[32,2,128]{2,1,0:T(2,128)} %get-tuple-element.33), channel_id=1, source_target_pairs={{0,2},{2,4},{4,6},{6,0},{1,3},{3,5},{5,7},{7,1},{8,10},{10,12},{12... | collective-permute-start | bytes 98312 | tf_op jit(solution)/shard_map/ppermute | solution.py:476
  69.6 3.7 %collective-permute-start.6 = (f32[32,2,128]{2,1,0:T(2,128)}, f32[32,2,128]{2,1,0:T(2,128)S(1)}, u32[]{:S(2)}, u32[]{:S(2)}) collective-permute-start(f32[32,2,128]{2,1,0:T(2,128)} %get-tuple-element.34), channel_id=1, source_target_pairs={{0,6},{2,0},{4,2},{6,4},{1,7},{3,1},{5,3},{7,5},{8,14},{10,8},{12,... | collective-permute-start | bytes 98312 | tf_op jit(solution)/shard_map/ppermute | solution.py:477
  73.2 9.6 %copy-start.3 = (f32[32,2,128]{2,1,0:T(2,128)}, f32[32,2,128]{2,1,0:T(2,128)S(1)}, u32[]{:S(2)}) copy-start(f32[32,2,128]{2,1,0:T(2,128)S(1)} %collective-permute-done.5.args_1_) | copy-start | bytes 98308
  73.3 9.5 %copy-start.4 = (f32[32,2,128]{2,1,0:T(2,128)}, f32[32,2,128]{2,1,0:T(2,128)S(1)}, u32[]{:S(2)}) copy-start(f32[32,2,128]{2,1,0:T(2,128)S(1)} %collective-permute-done.6.args_2_) | copy-start | bytes 98308
  76.6 6.2 %collective-permute-start.7 = (f32[32,2,128]{2,1,0:T(2,128)}, f32[32,2,128]{2,1,0:T(2,128)S(1)}, u32[]{:S(2)}, u32[]{:S(2)}) collective-permute-start(f32[32,2,128]{2,1,0:T(2,128)} %get-tuple-element.35), channel_id=1, source_target_pairs={{0,8},{8,16},{16,24},{24,0},{1,9},{9,17},{17,25},{25,1},{2,10},{10... | collective-permute-start | bytes 98312 | tf_op jit(solution)/shard_map/ppermute | solution.py:476
  77.6 5.3 %collective-permute-start.8 = (f32[32,2,128]{2,1,0:T(2,128)}, f32[32,2,128]{2,1,0:T(2,128)S(1)}, u32[]{:S(2)}, u32[]{:S(2)}) collective-permute-start(f32[32,2,128]{2,1,0:T(2,128)} %get-tuple-element.36), channel_id=1, source_target_pairs={{0,24},{8,0},{16,8},{24,16},{1,25},{9,1},{17,9},{25,17},{2,26},{10... | collective-permute-start | bytes 98312 | tf_op jit(solution)/shard_map/ppermute | solution.py:477
  82.8 0.6 copy-start.10
  83.4 0.6 copy-start.11
  86.9 8.5 %collective-permute-start.9 = (f32[4,128,128]{2,1,0:T(8,128)}, f32[4,128,128]{2,1,0:T(8,128)S(1)}, u32[]{:S(2)}, u32[]{:S(2)}) collective-permute-start(f32[4,128,128]{2,1,0:T(8,128)} %ends.4), channel_id=1, source_target_pairs={{0,1},{1,0},{2,3},{3,2},{4,5},{5,4},{6,7},{7,6},{8,9},{9,8},{10,11... | collective-permute-start | bytes 786440 | tf_op jit(solution)/shard_map/ppermute | solution.py:484
  95.4 0.7 copy-start.7
  100.1 3.4 %collective-permute-start.10 = (f32[16,2,64]{2,1,0:T(2,128)}, f32[16,2,64]{2,1,0:T(2,128)S(1)}, u32[]{:S(2)}, u32[]{:S(2)}) collective-permute-start(f32[16,2,64]{2,1,0:T(2,128)} %get-tuple-element.41), channel_id=1, source_target_pairs={{0,2},{2,4},{4,6},{6,0},{1,3},{3,5},{5,7},{7,1},{8,10},{10,12},{12... | collective-permute-start | bytes 24584 | tf_op jit(solution)/shard_map/ppermute | solution.py:476
  100.1 3.4 %collective-permute-start.11 = (f32[16,2,64]{2,1,0:T(2,128)}, f32[16,2,64]{2,1,0:T(2,128)S(1)}, u32[]{:S(2)}, u32[]{:S(2)}) collective-permute-start(f32[16,2,64]{2,1,0:T(2,128)} %get-tuple-element.42), channel_id=1, source_target_pairs={{0,6},{2,0},{4,2},{6,4},{1,7},{3,1},{5,3},{7,5},{8,14},{10,8},{12,... | collective-permute-start | bytes 24584 | tf_op jit(solution)/shard_map/ppermute | solution.py:477
  103.4 8.6 %copy-start.5 = (f32[16,2,64]{2,1,0:T(2,128)}, f32[16,2,64]{2,1,0:T(2,128)S(1)}, u32[]{:S(2)}) copy-start(f32[16,2,64]{2,1,0:T(2,128)S(1)} %collective-permute-done.10.args_1_) | copy-start | bytes 24580
  103.5 8.6 %copy-start.6 = (f32[16,2,64]{2,1,0:T(2,128)}, f32[16,2,64]{2,1,0:T(2,128)S(1)}, u32[]{:S(2)}) copy-start(f32[16,2,64]{2,1,0:T(2,128)S(1)} %collective-permute-done.11.args_2_) | copy-start | bytes 24580
  106.3 5.8 %collective-permute-start.12 = (f32[16,2,128]{2,1,0:T(2,128)}, f32[16,2,128]{2,1,0:T(2,128)S(1)}, u32[]{:S(2)}, u32[]{:S(2)}) collective-permute-start(f32[16,2,128]{2,1,0:T(2,128)} %get-tuple-element.43), channel_id=1, source_target_pairs={{0,8},{8,16},{16,24},{24,0},{1,9},{9,17},{17,25},{25,1},{2,10},{10... | collective-permute-start | bytes 49160 | tf_op jit(solution)/shard_map/ppermute | solution.py:476
  106.3 5.8 %collective-permute-start.13 = (f32[16,2,128]{2,1,0:T(2,128)}, f32[16,2,128]{2,1,0:T(2,128)S(1)}, u32[]{:S(2)}, u32[]{:S(2)}) collective-permute-start(f32[16,2,128]{2,1,0:T(2,128)} %get-tuple-element.44), channel_id=1, source_target_pairs={{0,24},{8,0},{16,8},{24,16},{1,25},{9,1},{17,9},{25,17},{2,26},{10... | collective-permute-start | bytes 49160 | tf_op jit(solution)/shard_map/ppermute | solution.py:477
  112.1 0.6 copy-start.13
  112.7 0.6 copy-start.14
  115.6 5.7 %collective-permute-start.14 = (f32[4,64,128]{2,1,0:T(8,128)}, f32[4,64,128]{2,1,0:T(8,128)S(1)}, u32[]{:S(2)}, u32[]{:S(2)}) collective-permute-start(f32[4,64,128]{2,1,0:T(8,128)} %ends.5), channel_id=1, source_target_pairs={{0,1},{1,0},{2,3},{3,2},{4,5},{5,4},{6,7},{7,6},{8,9},{9,8},{10,11... | collective-permute-start | bytes 393224 | tf_op jit(solution)/shard_map/ppermute | solution.py:484
  121.2 0.7 copy-start.12

commit v3 on v2

--- a/solution.py
+++ b/solution.py
@@ -86,10 +86,9 @@
         self.high, self.low = np_halves(full)
         edge = np.zeros((4, self.out))
         edge[:, :valid] = rim
-        self.rim = edge.astype(np.float32)
-        rim_high, rim_low = np_halves(edge)
-        zeros = np.zeros((4, self.out), rim_high.dtype)
-        self.rim_packed = np.concatenate([rim_high, rim_high, rim_low, zeros])
+        self.rim_high, self.rim_low = np_halves(edge)
+        zeros = np.zeros((4, self.out), self.rim_high.dtype)
+        self.rim_packed = np.concatenate([self.rim_high, self.rim_high, self.rim_low, zeros])
 
 
 def dot(a, b):
@@ -138,15 +137,13 @@
     )(x)
 
 
-def rows_kernel(sizes, top_ref, bottom_ref, rim_rows_ref, high_ref, low_ref, rim_ref, left_ref, right_ref):
+def rows_kernel(sizes, top_ref, bottom_ref, rim_rows_ref, high_ref, low_ref, rim_high_ref, rim_low_ref, left_ref, right_ref):
     z = sizes.z
 
     def across(ref, at):
         out = times(ref[...].reshape(z * 8, sizes.lanes), high_ref, low_ref)
-        for h in range(4):
-            column = rim_rows_ref[:, 8 * at : 8 * at + 8, h : h + 1].reshape(z * 8, 1)
-            out = out + column * rim_ref[h : h + 1]
-        return out.reshape(z, 8, sizes.out)
+        columns = rim_rows_ref[:, 8 * at : 8 * at + 8, :].reshape(z * 8, 4)
+        return (out + times(columns, rim_high_ref, rim_low_ref)).reshape(z, 8, sizes.out)
 
     top = across(top_ref, 0)
     bottom = across(bottom_ref, 1)
@@ -171,12 +168,13 @@
             whole(rim_rows.shape),
             whole(sizes.high.shape),
             whole(sizes.low.shape),
-            whole(sizes.rim.shape),
+            whole(sizes.rim_high.shape),
+            whole(sizes.rim_low.shape),
         ],
         out_specs=[whole(out.shape), whole(out.shape)],
         out_shape=[out, out],
         name="rows",
-    )(x, x, rim_rows, sizes.high, sizes.low, sizes.rim)
+    )(x, x, rim_rows, sizes.high, sizes.low, sizes.rim_high, sizes.rim_low)
 
 
 def across_planes(sizes, count, refs, work):
@@ -223,19 +221,18 @@
 
 
 def ends_kernel(sizes, *args):
-    refs, out_ref, work = args[:8], args[8], args[9]
-    across_planes(sizes, 4, refs, work)
-    for c in range(sizes.out // LANES):
-        lanes = slice(c * LANES, (c + 1) * LANES)
-        v = [work[p, c, EDGE : EDGE + sizes.x] for p in range(4)]
-
-        @pl.when(pl.program_id(0) == 0)
-        def _():
-            out_ref[0, :, lanes], out_ref[1, :, lanes] = for_left(*v[:3])
-
-        @pl.when(pl.program_id(0) == 1)
-        def _():
-            out_ref[2, :, lanes], out_ref[3, :, lanes] = for_right(*v)
+    data, tables, out_ref, work, combined = args[:5], args[5:8], args[8], args[9], args[10:]
+
+    def send(combine, picks, at):
+        for ref, made in zip(data, combined):
+            made[0], made[1] = combine(*[ref[k] for k in picks])
+        across_planes(sizes, 2, (*combined, *tables), work)
+        for k in range(2):
+            for c in range(sizes.out // LANES):
+                out_ref[at + k, :, c * LANES : (c + 1) * LANES] = work[k, c, EDGE : EDGE + sizes.x]
+
+    pl.when(pl.program_id(0) == 0)(lambda: send(for_left, (0, 1, 2), 0))
+    pl.when(pl.program_id(0) == 1)(lambda: send(for_right, (0, 1, 2, 3), 2))
 
 
 def stream_kernel(sizes, group, steps, more, *args):
@@ -322,8 +319,15 @@
         in_specs=across_specs(sizes, 4, lambda i: (i * last, 0, 0)),
         out_specs=whole(out.shape),
         out_shape=out,
-        scratch_shapes=[pltpu.VMEM((4, sizes.out // LANES, sizes.x + 2 * EDGE, LANES), jnp.float32)],
-        cost_estimate=cost(sizes, 8),
+        scratch_shapes=[
+            pltpu.VMEM((2, sizes.out // LANES, sizes.x + 2 * EDGE, LANES), jnp.float32),
+            pltpu.VMEM((2, sizes.x, sizes.lanes), jnp.float32),
+            pltpu.VMEM((2, 2, sizes.x), jnp.float32),
+            pltpu.VMEM((2, 2, sizes.x), jnp.float32),
+            pltpu.VMEM((2, 2, sizes.out), jnp.float32),
+            pltpu.VMEM((2, 2, sizes.out), jnp.float32),
+        ],
+        cost_estimate=cost(sizes, 4),
         name="ends",
     )(*operands, sizes.high, sizes.low, sizes.rim_packed)
 

time: 134 us -> 133 us (level)
    pallas_call x3, Pallas kernels: 9.93 us -> 8.53 us  [ends(): pl.pallas_call(functools.partial(ends_kernel, sizes), grid=(2,), in_specs...]
where the time goes in v3:
time: 133 us
  Pallas kernels  81.4 us (61%)
  waiting for transfers between devices  22.1 us (17%)
  starting transfers between devices  20.1 us (15%)
  local copies, waits for them, and re-layouts  8.42 us (6%)
    pallas_call x3, Pallas kernels, stream(): pl.pallas_call(functools.partial(stream_kernel, sizes, group, steps, more...  35.1 us
    ppermute x6, waiting for transfers between devices, exchange(): lax.ppermute(right, axis, [(i, (i + 1) % count) for i in range(count)])  15.1 us
    ppermute x6, starting transfers between devices, exchange(): lax.ppermute(left, axis, [(i, (i - 1) % count) for i in range(count)])  14.3 us
    pallas_call x3, Pallas kernels, edges(): pl.pallas_call(functools.partial(edges_kernel, sizes, count), grid=(sizes...  12.9 us
    pallas_call x1, Pallas kernels, place(): pl.pallas_call(functools.partial(place_kernel, count), grid=(z // 2 // co...  10.1 us
    pallas_call x3, Pallas kernels, ends(): pl.pallas_call(functools.partial(ends_kernel, sizes), grid=(2,), in_specs...  8.53 us
    pallas_call x3, Pallas kernels, rows(): pl.pallas_call(functools.partial(rows_kernel, sizes), grid=(1,), in_specs...  7.61 us
    pallas_call x3, Pallas kernels, finish(): pl.pallas_call(functools.partial(finish_kernel, sizes, more), grid=(min(2...  7.07 us
  transfers between devices with their start and end apart: 15, of which 11 were waited for; matrix products, arithmetic and copies ran while one was open for 0% of the time, Pallas kernels for 26%

profile of v3, /device:TPU:0, one launch (start us, length us, event | category | flops | bytes accessed | tf_op | source)
XLA Modules:
  0.0 132.6 jit_solution(18399546692226080364)
XLA Ops:
  0.0 7.8 %edges.3 = (f32[64,2,256]{2,1,0:T(2,128)}, f32[64,2,256]{2,1,0:T(2,128)}) custom-call(f32[64,256,256]{2,1,0:T(8,128)} %args_0_.6), custom_call_target="tpu_custom_call" | custom-call | tf_op jit(solution)/shard_map/edges/pallas_call | solution.py:130
  7.8 0.5 collective-permute-start
  8.3 1.9 %collective-permute-start.1 = (f32[64,2,256]{2,1,0:T(2,128)}, f32[64,2,256]{2,1,0:T(2,128)S(1)}, u32[]{:S(2)}, u32[]{:S(2)}) collective-permute-start(f32[64,2,256]{2,1,0:T(2,128)} %get-tuple-element.26), channel_id=1, source_target_pairs={{0,6},{2,0},{4,2},{6,4},{1,7},{3,1},{5,3},{7,5},{8,14},{10,8},{12,... | collective-permute-start | bytes 393224 | tf_op jit(solution)/shard_map/ppermute | solution.py:481
  10.2 2.9 %collective-permute-done.args_1_ = f32[64,2,256]{2,1,0:T(2,128)S(1)} collective-permute-done((f32[64,2,256]{2,1,0:T(2,128)}, f32[64,2,256]{2,1,0:T(2,128)S(1)}, u32[]{:S(2)}, u32[]{:S(2)}) %collective-permute-start) | collective-permute-done | bytes 131104 | tf_op jit(solution)/shard_map/ppermute | solution.py:480
  13.0 1.3 %collective-permute-done.1.args_2_ = f32[64,2,256]{2,1,0:T(2,128)S(1)} collective-permute-done((f32[64,2,256]{2,1,0:T(2,128)}, f32[64,2,256]{2,1,0:T(2,128)S(1)}, u32[]{:S(2)}, u32[]{:S(2)}) %collective-permute-start.1) | collective-permute-done | bytes 131104 | tf_op jit(solution)/shard_map/ppermute | solution.py:481
  14.6 1.2 copy.33.rim_rows_ref
  15.9 3.5 %rows.3 = (f32[64,2,256]{2,1,0:T(2,128)}, f32[64,2,256]{2,1,0:T(2,128)}) custom-call(f32[64,256,256]{2,1,0:T(8,128)} %args_0_.6, f32[64,256,256]{2,1,0:T(8,128)} %args_0_.6, f32[64,16,4]{2,1,0:T(8,128)} %copy.33.rim_rows_ref, bf16[256,256]{1,0:T(8,128)(2,1)} %constant.34.clone.high_ref.args_5_, bf16[256,256]{1,0:T(8,128)(2,1)} %constant.35.clone.low_ref.args_6_, ...), custom_call_target="tpu_custom_call" | custom-call | tf_op jit(solution)/shard_map/rows/pallas_call | solution.py:162
  19.3 1.6 %collective-permute-start.2 = (f32[64,2,256]{2,1,0:T(2,128)}, f32[64,2,256]{2,1,0:T(2,128)S(1)}, u32[]{:S(2)}, u32[]{:S(2)}) collective-permute-start(f32[64,2,256]{2,1,0:T(2,128)} %get-tuple-element.27), channel_id=1, source_target_pairs={{0,8},{8,16},{16,24},{24,0},{1,9},{9,17},{17,25},{25,1},{2,10},{10... | collective-permute-start | bytes 393224 | tf_op jit(solution)/shard_map/ppermute | solution.py:480
  21.0 2.2 %collective-permute-start.3 = (f32[64,2,256]{2,1,0:T(2,128)}, f32[64,2,256]{2,1,0:T(2,128)S(1)}, u32[]{:S(2)}, u32[]{:S(2)}) collective-permute-start(f32[64,2,256]{2,1,0:T(2,128)} %get-tuple-element.28), channel_id=1, source_target_pairs={{0,24},{8,0},{16,8},{24,16},{1,25},{9,1},{17,9},{25,17},{2,26},{10... | collective-permute-start | bytes 393224 | tf_op jit(solution)/shard_map/ppermute | solution.py:481
  23.2 4.5 %collective-permute-done.2.args_3_ = f32[64,2,256]{2,1,0:T(2,128)S(1)} collective-permute-done((f32[64,2,256]{2,1,0:T(2,128)}, f32[64,2,256]{2,1,0:T(2,128)S(1)}, u32[]{:S(2)}, u32[]{:S(2)}) %collective-permute-start.2) | collective-permute-done | bytes 131104 | tf_op jit(solution)/shard_map/ppermute | solution.py:480
  27.7 2.5 %collective-permute-done.3.args_4_ = f32[64,2,256]{2,1,0:T(2,128)S(1)} collective-permute-done((f32[64,2,256]{2,1,0:T(2,128)}, f32[64,2,256]{2,1,0:T(2,128)S(1)}, u32[]{:S(2)}, u32[]{:S(2)}) %collective-permute-start.3) | collective-permute-done | bytes 131104 | tf_op jit(solution)/shard_map/ppermute | solution.py:481
  30.2 0.6 copy-done.9
  30.8 3.8 %ends.3 = f32[4,256,256]{2,1,0:T(8,128)} custom-call(f32[64,256,256]{2,1,0:T(8,128)} %args_0_.6, f32[64,2,256]{2,1,0:T(2,128)} %copy-done, f32[64,2,256]{2,1,0:T(2,128)} %copy-done.1, f32[64,2,256]{2,1,0:T(2,128)} %copy-done.8, f32[64,2,256]{2,1,0:T(2,128)} %copy-done.9, bf16[256,256]{1,0:T(8,128)(2,1)} %constant.34.clone.high_ref.args_5_, ...), custom_call_target="tpu_custom_call" | custom-call | flops 536870912 | bytes 2097152 | tf_op jit(solution)/shard_map/ends/pallas_call | solution.py:316
  34.6 1.5 %collective-permute-start.4 = (f32[4,256,256]{2,1,0:T(8,128)}, f32[4,256,256]{2,1,0:T(8,128)S(1)}, u32[]{:S(2)}, u32[]{:S(2)}) collective-permute-start(f32[4,256,256]{2,1,0:T(8,128)} %ends.3), channel_id=1, source_target_pairs={{0,1},{1,0},{2,3},{3,2},{4,5},{5,4},{6,7},{7,6},{8,9},{9,8},{10,11... | collective-permute-start | bytes 3145736 | tf_op jit(solution)/shard_map/ppermute | solution.py:488
  36.1 25.1 %stream.3 = (f32[64,256,256]{2,1,0:T(8,128)}, f32[32,128,256]{2,1,0:T(8,128)}) custom-call(f32[64,256,256]{2,1,0:T(8,128)} %args_0_.6, f32[64,2,256]{2,1,0:T(2,128)} %copy-done, f32[64,2,256]{2,1,0:T(2,128)} %copy-done.1, f32[64,2,256]{2,1,0:T(2,128)} %copy-done.8, f32[64,2,256]{2,1,0:T(2,128)} %copy-done.9, ...), custom_call_target="tpu_custom_call" | custom-call | flops 8589934592 | bytes 33554432 | tf_op jit(solution)/shard_map/stream/pallas_call | solution.py:345
  61.2 1.0 copy-done.2
  62.3 3.4 %finish.3 = (f32[64,256,256]{2,1,0:T(8,128)}, f32[32,128,256]{2,1,0:T(8,128)}) custom-call(f32[4,256,256]{2,1,0:T(8,128)} %copy-done.2, f32[64,256,256]{2,1,0:T(8,128)} %get-tuple-element.29.t_ref, f32[32,128,256]{2,1,0:T(8,128)} %get-tuple-element.30.rest_0_), custom_call_target="tpu_custom_call", output_to_operand_aliasing={{0}: (1, {}), {1}: (2, {})} | custom-call | tf_op jit(solution)/shard_map/finish/pallas_call | solution.py:402
  65.6 3.2 %edges.4 = (f32[32,2,128]{2,1,0:T(2,128)}, f32[32,2,128]{2,1,0:T(2,128)}) custom-call(f32[32,128,256]{2,1,0:T(8,128)} %get-tuple-element.32.x_ref.top_ref.bottom_ref.args_0_), custom_call_target="tpu_custom_call" | custom-call | tf_op jit(solution)/shard_map/edges/pallas_call | solution.py:130
  68.8 1.7 %collective-permute-start.6 = (f32[32,2,128]{2,1,0:T(2,128)}, f32[32,2,128]{2,1,0:T(2,128)S(1)}, u32[]{:S(2)}, u32[]{:S(2)}) collective-permute-start(f32[32,2,128]{2,1,0:T(2,128)} %get-tuple-element.34), channel_id=1, source_target_pairs={{0,6},{2,0},{4,2},{6,4},{1,7},{3,1},{5,3},{7,5},{8,14},{10,8},{12,... | collective-permute-start | bytes 98312 | tf_op jit(solution)/shard_map/ppermute | solution.py:481
  70.5 1.8 %collective-permute-done.5.args_1_ = f32[32,2,128]{2,1,0:T(2,128)S(1)} collective-permute-done((f32[32,2,128]{2,1,0:T(2,128)}, f32[32,2,128]{2,1,0:T(2,128)S(1)}, u32[]{:S(2)}, u32[]{:S(2)}) %collective-permute-start.5) | collective-permute-done | bytes 32800 | tf_op jit(solution)/shard_map/ppermute | solution.py:480
  72.6 1.0 copy.34.rim_rows_ref
  73.6 2.3 %rows.4 = (f32[32,2,128]{2,1,0:T(2,128)}, f32[32,2,128]{2,1,0:T(2,128)}) custom-call(f32[32,128,256]{2,1,0:T(8,128)} %get-tuple-element.32.x_ref.top_ref.bottom_ref.args_0_, f32[32,128,256]{2,1,0:T(8,128)} %get-tuple-element.32.x_ref.top_ref.bottom_ref.args_0_, f32[32,16,4]{2,1,0:T(8,128)} %copy.34.rim_rows_ref, ...), custom_call_target="tpu_custom_call" | custom-call | tf_op jit(solution)/shard_map/rows/pallas_call | solution.py:162
  75.9 1.0 collective-permute-start.7
  76.9 2.9 %collective-permute-start.8 = (f32[32,2,128]{2,1,0:T(2,128)}, f32[32,2,128]{2,1,0:T(2,128)S(1)}, u32[]{:S(2)}, u32[]{:S(2)}) collective-permute-start(f32[32,2,128]{2,1,0:T(2,128)} %get-tuple-element.36), channel_id=1, source_target_pairs={{0,24},{8,0},{16,8},{24,16},{1,25},{9,1},{17,9},{25,17},{2,26},{10... | collective-permute-start | bytes 98312 | tf_op jit(solution)/shard_map/ppermute | solution.py:481
  79.7 2.4 %collective-permute-done.7.args_3_ = f32[32,2,128]{2,1,0:T(2,128)S(1)} collective-permute-done((f32[32,2,128]{2,1,0:T(2,128)}, f32[32,2,128]{2,1,0:T(2,128)S(1)}, u32[]{:S(2)}, u32[]{:S(2)}) %collective-permute-start.7) | collective-permute-done | bytes 32800 | tf_op jit(solution)/shard_map/ppermute | solution.py:480
  82.1 0.6 copy-done.10
  82.7 0.6 copy-done.11
  83.3 2.6 %ends.4 = f32[4,128,128]{2,1,0:T(8,128)} custom-call(f32[32,128,256]{2,1,0:T(8,128)} %get-tuple-element.32.x_ref.top_ref.bottom_ref.args_0_, f32[32,2,128]{2,1,0:T(2,128)} %copy-done.3, f32[32,2,128]{2,1,0:T(2,128)} %copy-done.4, f32[32,2,128]{2,1,0:T(2,128)} %copy-done.10, f32[32,2,128]{2,1,0:T(2,128)} %copy-done.11, ...), custom_call_target="tpu_custom_call" | custom-call | flops 134217728 | bytes 786432 | tf_op jit(solution)/shard_map/ends/pallas_call | solution.py:316
  86.4 7.0 %stream.4 = (f32[32,128,128]{2,1,0:T(8,128)}, f32[16,64,128]{2,1,0:T(8,128)}) custom-call(f32[32,128,256]{2,1,0:T(8,128)} %get-tuple-element.32.x_ref.top_ref.bottom_ref.args_0_, f32[32,2,128]{2,1,0:T(2,128)} %copy-done.3, f32[32,2,128]{2,1,0:T(2,128)} %copy-done.4, f32[32,2,128]{2,1,0:T(2,128)} %copy-done.10, f32[32,2,128]{2,1,0:T(2,128)} %copy-done.11, ...), custom_call_target="tpu_custom_call" | custom-call | flops 1073741824 | bytes 6291456 | tf_op jit(solution)/shard_map/stream/pallas_call | solution.py:345
  93.4 0.9 collective-permute-done.9.z_ref
  94.4 0.7 copy-done.7
  95.1 2.0 %finish.4 = (f32[32,128,128]{2,1,0:T(8,128)}, f32[16,64,128]{2,1,0:T(8,128)}) custom-call(f32[4,128,128]{2,1,0:T(8,128)} %copy-done.7, f32[32,128,128]{2,1,0:T(8,128)} %get-tuple-element.37.t_ref, f32[16,64,128]{2,1,0:T(8,128)} %get-tuple-element.38.rest_0_), custom_call_target="tpu_custom_call", output_to_operand_aliasing={{0}: (1, {}), {1}: (2, {})} | custom-call | tf_op jit(solution)/shard_map/finish/pallas_call | solution.py:402
  97.0 2.0 %edges.5 = (f32[16,2,64]{2,1,0:T(2,128)}, f32[16,2,64]{2,1,0:T(2,128)}) custom-call(f32[16,64,128]{2,1,0:T(8,128)} %get-tuple-element.40.x_ref.top_ref.bottom_ref.args_0_), custom_call_target="tpu_custom_call" | custom-call | tf_op jit(solution)/shard_map/edges/pallas_call | solution.py:130
  99.0 1.7 %collective-permute-start.11 = (f32[16,2,64]{2,1,0:T(2,128)}, f32[16,2,64]{2,1,0:T(2,128)S(1)}, u32[]{:S(2)}, u32[]{:S(2)}) collective-permute-start(f32[16,2,64]{2,1,0:T(2,128)} %get-tuple-element.42), channel_id=1, source_target_pairs={{0,6},{2,0},{4,2},{6,4},{1,7},{3,1},{5,3},{7,5},{8,14},{10,8},{12,... | collective-permute-start | bytes 24584 | tf_op jit(solution)/shard_map/ppermute | solution.py:481
  100.8 1.6 %collective-permute-done.10.args_1_ = f32[16,2,64]{2,1,0:T(2,128)S(1)} collective-permute-done((f32[16,2,64]{2,1,0:T(2,128)}, f32[16,2,64]{2,1,0:T(2,128)S(1)}, u32[]{:S(2)}, u32[]{:S(2)}) %collective-permute-start.10) | collective-permute-done | bytes 8224 | tf_op jit(solution)/shard_map/ppermute | solution.py:480
  102.6 0.8 copy.35.rim_rows_ref
  103.4 1.9 %rows.5 = (f32[16,2,128]{2,1,0:T(2,128)}, f32[16,2,128]{2,1,0:T(2,128)}) custom-call(f32[16,64,128]{2,1,0:T(8,128)} %get-tuple-element.40.x_ref.top_ref.bottom_ref.args_0_, f32[16,64,128]{2,1,0:T(8,128)} %get-tuple-element.40.x_ref.top_ref.bottom_ref.args_0_, f32[16,16,4]{2,1,0:T(8,128)} %copy.35.rim_rows_ref, ...), custom_call_target="tpu_custom_call" | custom-call | tf_op jit(solution)/shard_map/rows/pallas_call | solution.py:162
  105.3 3.8 %collective-permute-start.13 = (f32[16,2,128]{2,1,0:T(2,128)}, f32[16,2,128]{2,1,0:T(2,128)S(1)}, u32[]{:S(2)}, u32[]{:S(2)}) collective-permute-start(f32[16,2,128]{2,1,0:T(2,128)} %get-tuple-element.44), channel_id=1, source_target_pairs={{0,24},{8,0},{16,8},{24,16},{1,25},{9,1},{17,9},{25,17},{2,26},{10... | collective-permute-start | bytes 49160 | tf_op jit(solution)/shard_map/ppermute | solution.py:481
  109.1 2.0 %collective-permute-done.12.args_3_ = f32[16,2,128]{2,1,0:T(2,128)S(1)} collective-permute-done((f32[16,2,128]{2,1,0:T(2,128)}, f32[16,2,128]{2,1,0:T(2,128)S(1)}, u32[]{:S(2)}, u32[]{:S(2)}) %collective-permute-start.12) | collective-permute-done | bytes 16416 | tf_op jit(solution)/shard_map/ppermute | solution.py:480
  111.1 0.6 copy-done.13
  111.7 0.6 copy-done.14
  112.3 2.2 %ends.5 = f32[4,64,128]{2,1,0:T(8,128)} custom-call(f32[16,64,128]{2,1,0:T(8,128)} %get-tuple-element.40.x_ref.top_ref.bottom_ref.args_0_, f32[16,2,64]{2,1,0:T(2,128)} %copy-done.5, f32[16,2,64]{2,1,0:T(2,128)} %copy-done.6, f32[16,2,128]{2,1,0:T(2,128)} %copy-done.13, f32[16,2,128]{2,1,0:T(2,128)} %copy-done.14, ...), custom_call_target="tpu_custom_call" | custom-call | flops 33554432 | bytes 262144 | tf_op jit(solution)/shard_map/ends/pallas_call | solution.py:316
  114.5 0.6 collective-permute-start.14
  115.1 3.0 %stream.5.t_ref = f32[16,64,128]{2,1,0:T(8,128)} custom-call(f32[16,64,128]{2,1,0:T(8,128)} %get-tuple-element.40.x_ref.top_ref.bottom_ref.args_0_, f32[16,2,64]{2,1,0:T(2,128)} %copy-done.5, f32[16,2,64]{2,1,0:T(2,128)} %copy-done.6, f32[16,2,128]{2,1,0:T(2,128)} %copy-done.13, f32[16,2,128]{2,1,0:T(2,128)} %copy-done.14, ...), custom_call_target="tpu_custom_call" | custom-call | flops 134217728 | bytes 1048576 | tf_op jit(solution)/shard_map/stream/pallas_call | solution.py:345
  118.1 2.1 %collective-permute-done.14.z_ref = f32[4,64,128]{2,1,0:T(8,128)S(1)} collective-permute-done((f32[4,64,128]{2,1,0:T(8,128)}, f32[4,64,128]{2,1,0:T(8,128)S(1)}, u32[]{:S(2)}, u32[]{:S(2)}) %collective-permute-start.14) | collective-permute-done | bytes 131104 | tf_op jit(solution)/shard_map/ppermute | solution.py:488
  120.1 0.7 copy-done.12
  120.8 1.7 %finish.5.inner_ref = f32[16,64,128]{2,1,0:T(8,128)} custom-call(f32[4,64,128]{2,1,0:T(8,128)} %copy-done.12, f32[16,64,128]{2,1,0:T(8,128)} %stream.5.t_ref), custom_call_target="tpu_custom_call", output_to_operand_aliasing={{}: (1, {})} | custom-call | tf_op jit(solution)/shard_map/finish/pallas_call | solution.py:402
  122.5 10.1 %place.1 = f32[32,2,256,256]{3,2,1,0:T(8,128)} custom-call(f32[32,2,256,256]{3,2,1,0:T(8,128)} %bitcast.8, f32[32,128,128]{2,1,0:T(8,128)} %get-tuple-element.39.middle_ref, f32[16,64,128]{2,1,0:T(8,128)} %finish.5.inner_ref, bf16[128,256]{1,0:T(8,128)(2,1)} %constant.49.clone.outer_table_ref, ...), custom_call_target="tpu_custom_call", output_to_operand_aliasing={{}: (0, {})} | custom-call | tf_op jit(solution)/shard_map/place/pallas_call | solution.py:457
  (37 shorter events, 1.2 us)
Async XLA Ops:
  7.8 5.3 %collective-permute-start = (f32[64,2,256]{2,1,0:T(2,128)}, f32[64,2,256]{2,1,0:T(2,128)S(1)}, u32[]{:S(2)}, u32[]{:S(2)}) collective-permute-start(f32[64,2,256]{2,1,0:T(2,128)} %get-tuple-element.25), channel_id=1, source_target_pairs={{0,2},{2,4},{4,6},{6,0},{1,3},{3,5},{5,7},{7,1},{8,10},{10,12},{12... | collective-permute-start | bytes 393224 | tf_op jit(solution)/shard_map/ppermute | solution.py:480
  8.3 6.1 %collective-permute-start.1 = (f32[64,2,256]{2,1,0:T(2,128)}, f32[64,2,256]{2,1,0:T(2,128)S(1)}, u32[]{:S(2)}, u32[]{:S(2)}) collective-permute-start(f32[64,2,256]{2,1,0:T(2,128)} %get-tuple-element.26), channel_id=1, source_target_pairs={{0,6},{2,0},{4,2},{6,4},{1,7},{3,1},{5,3},{7,5},{8,14},{10,8},{12,... | collective-permute-start | bytes 393224 | tf_op jit(solution)/shard_map/ppermute | solution.py:481
  13.0 6.3 %copy-start = (f32[64,2,256]{2,1,0:T(2,128)}, f32[64,2,256]{2,1,0:T(2,128)S(1)}, u32[]{:S(2)}) copy-start(f32[64,2,256]{2,1,0:T(2,128)S(1)} %collective-permute-done.args_1_) | copy-start | bytes 393220
  14.4 5.0 %copy-start.1 = (f32[64,2,256]{2,1,0:T(2,128)}, f32[64,2,256]{2,1,0:T(2,128)S(1)}, u32[]{:S(2)}) copy-start(f32[64,2,256]{2,1,0:T(2,128)S(1)} %collective-permute-done.1.args_2_) | copy-start | bytes 393220
  19.3 8.4 %collective-permute-start.2 = (f32[64,2,256]{2,1,0:T(2,128)}, f32[64,2,256]{2,1,0:T(2,128)S(1)}, u32[]{:S(2)}, u32[]{:S(2)}) collective-permute-start(f32[64,2,256]{2,1,0:T(2,128)} %get-tuple-element.27), channel_id=1, source_target_pairs={{0,8},{8,16},{16,24},{24,0},{1,9},{9,17},{17,25},{25,1},{2,10},{10... | collective-permute-start | bytes 393224 | tf_op jit(solution)/shard_map/ppermute | solution.py:480
  21.0 9.2 %collective-permute-start.3 = (f32[64,2,256]{2,1,0:T(2,128)}, f32[64,2,256]{2,1,0:T(2,128)S(1)}, u32[]{:S(2)}, u32[]{:S(2)}) collective-permute-start(f32[64,2,256]{2,1,0:T(2,128)} %get-tuple-element.28), channel_id=1, source_target_pairs={{0,24},{8,0},{16,8},{24,16},{1,25},{9,1},{17,9},{25,17},{2,26},{10... | collective-permute-start | bytes 393224 | tf_op jit(solution)/shard_map/ppermute | solution.py:481
  27.7 2.5 %copy-start.8 = (f32[64,2,256]{2,1,0:T(2,128)}, f32[64,2,256]{2,1,0:T(2,128)S(1)}, u32[]{:S(2)}) copy-start(f32[64,2,256]{2,1,0:T(2,128)S(1)} %collective-permute-done.2.args_3_) | copy-start | bytes 393220
  30.2 0.6 copy-start.9
  34.6 26.6 %collective-permute-start.4 = (f32[4,256,256]{2,1,0:T(8,128)}, f32[4,256,256]{2,1,0:T(8,128)S(1)}, u32[]{:S(2)}, u32[]{:S(2)}) collective-permute-start(f32[4,256,256]{2,1,0:T(8,128)} %ends.3), channel_id=1, source_target_pairs={{0,1},{1,0},{2,3},{3,2},{4,5},{5,4},{6,7},{7,6},{8,9},{9,8},{10,11... | collective-permute-start | bytes 3145736 | tf_op jit(solution)/shard_map/ppermute | solution.py:488
  61.2 1.0 copy-start.2
  68.8 3.6 %collective-permute-start.5 = (f32[32,2,128]{2,1,0:T(2,128)}, f32[32,2,128]{2,1,0:T(2,128)S(1)}, u32[]{:S(2)}, u32[]{:S(2)}) collective-permute-start(f32[32,2,128]{2,1,0:T(2,128)} %get-tuple-element.33), channel_id=1, source_target_pairs={{0,2},{2,4},{4,6},{6,0},{1,3},{3,5},{5,7},{7,1},{8,10},{10,12},{12... | collective-permute-start | bytes 98312 | tf_op jit(solution)/shard_map/ppermute | solution.py:480
  68.8 3.7 %collective-permute-start.6 = (f32[32,2,128]{2,1,0:T(2,128)}, f32[32,2,128]{2,1,0:T(2,128)S(1)}, u32[]{:S(2)}, u32[]{:S(2)}) collective-permute-start(f32[32,2,128]{2,1,0:T(2,128)} %get-tuple-element.34), channel_id=1, source_target_pairs={{0,6},{2,0},{4,2},{6,4},{1,7},{3,1},{5,3},{7,5},{8,14},{10,8},{12,... | collective-permute-start | bytes 98312 | tf_op jit(solution)/shard_map/ppermute | solution.py:481
  72.4 9.7 %copy-start.3 = (f32[32,2,128]{2,1,0:T(2,128)}, f32[32,2,128]{2,1,0:T(2,128)S(1)}, u32[]{:S(2)}) copy-start(f32[32,2,128]{2,1,0:T(2,128)S(1)} %collective-permute-done.5.args_1_) | copy-start | bytes 98308
  72.5 9.6 %copy-start.4 = (f32[32,2,128]{2,1,0:T(2,128)}, f32[32,2,128]{2,1,0:T(2,128)S(1)}, u32[]{:S(2)}) copy-start(f32[32,2,128]{2,1,0:T(2,128)S(1)} %collective-permute-done.6.args_2_) | copy-start | bytes 98308
  75.9 6.2 %collective-permute-start.7 = (f32[32,2,128]{2,1,0:T(2,128)}, f32[32,2,128]{2,1,0:T(2,128)S(1)}, u32[]{:S(2)}, u32[]{:S(2)}) collective-permute-start(f32[32,2,128]{2,1,0:T(2,128)} %get-tuple-element.35), channel_id=1, source_target_pairs={{0,8},{8,16},{16,24},{24,0},{1,9},{9,17},{17,25},{25,1},{2,10},{10... | collective-permute-start | bytes 98312 | tf_op jit(solution)/shard_map/ppermute | solution.py:480
  76.9 5.2 %collective-permute-start.8 = (f32[32,2,128]{2,1,0:T(2,128)}, f32[32,2,128]{2,1,0:T(2,128)S(1)}, u32[]{:S(2)}, u32[]{:S(2)}) collective-permute-start(f32[32,2,128]{2,1,0:T(2,128)} %get-tuple-element.36), channel_id=1, source_target_pairs={{0,24},{8,0},{16,8},{24,16},{1,25},{9,1},{17,9},{25,17},{2,26},{10... | collective-permute-start | bytes 98312 | tf_op jit(solution)/shard_map/ppermute | solution.py:481
  82.1 0.6 copy-start.10
  82.7 0.6 copy-start.11
  85.9 8.5 %collective-permute-start.9 = (f32[4,128,128]{2,1,0:T(8,128)}, f32[4,128,128]{2,1,0:T(8,128)S(1)}, u32[]{:S(2)}, u32[]{:S(2)}) collective-permute-start(f32[4,128,128]{2,1,0:T(8,128)} %ends.4), channel_id=1, source_target_pairs={{0,1},{1,0},{2,3},{3,2},{4,5},{5,4},{6,7},{7,6},{8,9},{9,8},{10,11... | collective-permute-start | bytes 786440 | tf_op jit(solution)/shard_map/ppermute | solution.py:488
  94.4 0.7 copy-start.7
  99.0 3.4 %collective-permute-start.10 = (f32[16,2,64]{2,1,0:T(2,128)}, f32[16,2,64]{2,1,0:T(2,128)S(1)}, u32[]{:S(2)}, u32[]{:S(2)}) collective-permute-start(f32[16,2,64]{2,1,0:T(2,128)} %get-tuple-element.41), channel_id=1, source_target_pairs={{0,2},{2,4},{4,6},{6,0},{1,3},{3,5},{5,7},{7,1},{8,10},{10,12},{12... | collective-permute-start | bytes 24584 | tf_op jit(solution)/shard_map/ppermute | solution.py:480
  99.0 3.4 %collective-permute-start.11 = (f32[16,2,64]{2,1,0:T(2,128)}, f32[16,2,64]{2,1,0:T(2,128)S(1)}, u32[]{:S(2)}, u32[]{:S(2)}) collective-permute-start(f32[16,2,64]{2,1,0:T(2,128)} %get-tuple-element.42), channel_id=1, source_target_pairs={{0,6},{2,0},{4,2},{6,4},{1,7},{3,1},{5,3},{7,5},{8,14},{10,8},{12,... | collective-permute-start | bytes 24584 | tf_op jit(solution)/shard_map/ppermute | solution.py:481
  102.4 8.7 %copy-start.5 = (f32[16,2,64]{2,1,0:T(2,128)}, f32[16,2,64]{2,1,0:T(2,128)S(1)}, u32[]{:S(2)}) copy-start(f32[16,2,64]{2,1,0:T(2,128)S(1)} %collective-permute-done.10.args_1_) | copy-start | bytes 24580
  102.4 8.7 %copy-start.6 = (f32[16,2,64]{2,1,0:T(2,128)}, f32[16,2,64]{2,1,0:T(2,128)S(1)}, u32[]{:S(2)}) copy-start(f32[16,2,64]{2,1,0:T(2,128)S(1)} %collective-permute-done.11.args_2_) | copy-start | bytes 24580
  105.3 5.8 %collective-permute-start.12 = (f32[16,2,128]{2,1,0:T(2,128)}, f32[16,2,128]{2,1,0:T(2,128)S(1)}, u32[]{:S(2)}, u32[]{:S(2)}) collective-permute-start(f32[16,2,128]{2,1,0:T(2,128)} %get-tuple-element.43), channel_id=1, source_target_pairs={{0,8},{8,16},{16,24},{24,0},{1,9},{9,17},{17,25},{25,1},{2,10},{10... | collective-permute-start | bytes 49160 | tf_op jit(solution)/shard_map/ppermute | solution.py:480
  105.3 5.8 %collective-permute-start.13 = (f32[16,2,128]{2,1,0:T(2,128)}, f32[16,2,128]{2,1,0:T(2,128)S(1)}, u32[]{:S(2)}, u32[]{:S(2)}) collective-permute-start(f32[16,2,128]{2,1,0:T(2,128)} %get-tuple-element.44), channel_id=1, source_target_pairs={{0,24},{8,0},{16,8},{24,16},{1,25},{9,1},{17,9},{25,17},{2,26},{10... | collective-permute-start | bytes 49160 | tf_op jit(solution)/shard_map/ppermute | solution.py:481
  111.1 0.6 copy-start.13
  111.7 0.6 copy-start.14
  114.5 5.7 %collective-permute-start.14 = (f32[4,64,128]{2,1,0:T(8,128)}, f32[4,64,128]{2,1,0:T(8,128)S(1)}, u32[]{:S(2)}, u32[]{:S(2)}) collective-permute-start(f32[4,64,128]{2,1,0:T(8,128)} %ends.5), channel_id=1, source_target_pairs={{0,1},{1,0},{2,3},{3,2},{4,5},{5,4},{6,7},{7,6},{8,9},{9,8},{10,11... | collective-permute-start | bytes 393224 | tf_op jit(solution)/shard_map/ppermute | solution.py:488
  120.1 0.7 copy-start.12
